TPU v7x, 256 devices: a whole 4x4x8 slice. The times are simulated.
256 devices in a mesh: state: 8 (over z), act: 32 (over x, y, core).
Axes of the slice: x: 4, y: 4, z: 8, core: 2. Of those that a mesh axis runs over, the one named last changes fastest.
Arguments:
- state_features: bfloat16 [768, 2048], P('state', 'act'), may hold values from -6 to 6
- action_features: bfloat16 [768, 256, 2048], P('state', 'act'), may hold values from -240 to 240
- targets: float32 [768], P('state'), may hold values from -12 to 12
- w_hidden: bfloat16 [2048, 2048], replicated, may hold values from -0.125 to 0.125
- w_head: float32 [2048], replicated, may hold values from -7 to 7
Outputs:
- grad_hidden: float32 [2048, 2048], P(('state', 'act'))
- grad_head: float32 [2048], replicated
- log_partition: float32 [768], P('state')
- mean_loss: float32 [], replicated
All inputs are finite; a program needn't handle non-finite values.
Results may differ from a plain program's by a relative error of at most 0.006.
Values may be sent and summed in bfloat16 or wider, within the bound.
A program may use at most 128 MiB of HBM per device.

v0:
```python
import functools

import jax
import jax.numpy as jnp
from jax import lax
from jax.sharding import Mesh
from jax.sharding import PartitionSpec as P

ACT = ("act_0", "act_1", "act_2")
STATE_ACT = ("state", "act_0", "act_1", "act_2")


norm_epsilon = 1e-06
penalty_weight = 2.0


def sent_to_all(value, axis):
    copies = jnp.broadcast_to(value, (lax.axis_size(axis), *value.shape))
    return lax.all_to_all(copies, axis, split_axis=0, concat_axis=0, tiled=True)


def joined_along(parts, dim):
    parts = jnp.moveaxis(parts, 0, dim)
    dims = parts.shape
    return parts.reshape(*dims[:dim], dims[dim] * dims[dim + 1], *dims[dim + 2 :])


def collect(value, axis, dim):
    parts = sent_to_all(value, axis)
    return joined_along(parts, dim)


def taken_together(value, axis):
    everything = sent_to_all(value, axis)
    return jnp.max(everything, axis=0)


def of_everyone(value, axis):
    everything = sent_to_all(value, axis)
    return jnp.sum(everything, axis=0)


def split_up(value, dim, count):
    dims = value.shape
    parts = value.reshape(*dims[:dim], count, dims[dim] // count, *dims[dim + 1 :])
    return jnp.moveaxis(parts, dim, 0)


def sum_at_owner(value, axis, dim):
    count = lax.axis_size(axis)
    parts = lax.all_to_all(split_up(value, dim, count), axis, 0, 0, tiled=True)
    return jnp.sum(parts, axis=0)


def over_axes(value, axes):
    return functools.reduce(lax.psum, axes, value)


def body(state_features, action_features, targets, w_hidden, w_head):
    states_here, actions_here, width = action_features.shape
    state_count = lax.axis_size("state")
    states_total = states_here * state_count
    whole_states = collect(state_features, ACT, 1)
    mixture = whole_states.astype(jnp.float32)[:, None, :] + action_features.astype(jnp.float32)
    normed = (
        mixture * lax.rsqrt(jnp.mean(mixture * mixture, -1, keepdims=True) + norm_epsilon)
    ).astype(jnp.bfloat16)
    flat_rows = normed.reshape(-1, width)
    preact = jnp.dot(flat_rows, w_hidden, preferred_element_type=jnp.float32)
    sigmoid_pre = jax.nn.sigmoid(preact)
    head_input = flat_rows.astype(jnp.float32) + preact * sigmoid_pre
    scores = jnp.sum(head_input * w_head, -1).reshape(states_here, actions_here)
    row_max = jnp.max(scores, -1)
    global_max = taken_together(row_max, ACT)
    local_sum = jnp.sum(jnp.exp(scores - global_max[:, None]), -1)
    log_partition = global_max + jnp.log(of_everyone(local_sum, ACT))
    softmax_weight = jnp.exp(scores - log_partition[:, None])
    action_index = lax.axis_index(ACT) * actions_here + jnp.arange(actions_here, dtype=jnp.int32)
    is_data = (action_index == 0)[None, :]
    bellman_gap = scores - targets[:, None]
    score_grad = penalty_weight * softmax_weight + jnp.where(
        is_data, bellman_gap - penalty_weight, 0.0
    )
    loss_terms = jnp.where(
        is_data,
        penalty_weight * (log_partition[:, None] - scores) + 0.5 * bellman_gap * bellman_gap,
        0.0,
    )
    grad_flat = score_grad.reshape(-1)
    head_local = jnp.sum(grad_flat[:, None] * head_input, 0)
    back_grad = (
        grad_flat[:, None] * w_head * (sigmoid_pre + preact * sigmoid_pre * (1.0 - sigmoid_pre))
    ).astype(jnp.bfloat16)
    grad_slab = lax.psum_scatter(
        lax.dot_general(
            flat_rows, back_grad, (((0,), (0,)), ((), ())), preferred_element_type=jnp.float32
        ),
        "state",
        scatter_dimension=0,
        tiled=True,
    )
    grad_hidden = sum_at_owner(grad_slab, ACT, 0)
    grad_head, loss_sum = (
        over_axes(head_local, STATE_ACT),
        over_axes(jnp.sum(loss_terms), STATE_ACT),
    )
    return (grad_hidden, grad_head, log_partition, loss_sum / states_total)


def solution(mesh):
    finer = Mesh(
        mesh.devices.reshape(mesh.shape["state"], 4, 4, 2), ("state", "act_0", "act_1", "act_2")
    )
    placed = (P("state", ACT), P("state", ACT, None), P("state"), P(), P())
    return jax.shard_map(
        body,
        mesh=finer,
        in_specs=placed,
        out_specs=(P(STATE_ACT, None), P(), P("state"), P()),
        check_vma=False,
    )
```

profile of v0, /device:TPU:1, one launch (start us, length us, event | category | flops | bytes accessed | tf_op | source)
XLA Modules:
  0.0 324.3 jit_solution(5015506502604255950)
XLA Ops:
  7.2 0.0 copy-start
  7.2 0.0 copy-start.3
  7.2 1.0 broadcast_in_dim.38
  8.2 20.0 %all_to_all.22 = bf16[32,96,64]{1,2,0:T(8,128)(2,1)S(1)} all-to-all(bf16[32,96,64]{1,2,0:T(8,128)(2,1)S(1)} %broadcast_in_dim.38), channel_id=1, replica_groups=mesh['state'=8,'act_0'=4,'act_1'=4,'act_2'=2] {'act_0','act_1','act_2'}, dimensions={0} | all-to-all | bytes 786432 | tf_op jit(solution)/shard_map/all_to_all | solution.py:19
  28.1 1.1 convert_element_type.33
  29.2 2.5 copy.19
  31.7 0.0 copy-done
  31.7 2.0 multiply_reduce_fusion.2
  33.8 0.1 copy.20
  33.8 0.1 copy.21
  33.9 0.0 copy-done.3
  33.9 0.0 copy-start.1
  34.0 13.4 %multiply_reduce_fusion.1 = (f32[768]{0:T(1024)S(1)}, f32[768,2048]{1,0:T(8,128)}) fusion(f32[2048]{0:T(1024)S(1)} %copy-done.3, f32[96,8]{1,0:T(8,128)S(1)} %copy.21, bf16[96,8,2048]{2,1,0:T(8,128)(2,1)S(1)} %copy-done, f32[96,2048]{1,0:T(8,128)} %copy.19, bf16[2048,2048]{1,0:T(8,128)(2,1)} %param.8), kind=kOutput, calls=%fused_computation.2 | convolution fusion | flops 6467615744 | bytes 18626560 | tf_op jit(solution)/shard_map/dot_general | solution.py:69
  47.3 0.1 reshape.91
  47.4 0.1 reduce_max.18
  47.5 0.6 broadcast_in_dim.39
  48.2 3.6 %all-to-all-start.1 = ((f32[32,1,96]{2,1,0:T(1,128)}), f32[32,1,96]{2,1,0:T(1,128)S(1)}, u32[]{:S(2)}, u32[]{:S(2)}) async-start(f32[32,1,96]{2,1,0:T(1,128)} %broadcast_in_dim.39), calls=%async_computation.1 | async-start | bytes 32768 | tf_op jit(solution)/shard_map/all_to_all | solution.py:19
  51.8 6.9 %all-to-all-done.1 = f32[32,1,96]{2,1,0:T(1,128)S(1)} async-done(((f32[32,1,96]{2,1,0:T(1,128)}), f32[32,1,96]{2,1,0:T(1,128)S(1)}, u32[]{:S(2)}, u32[]{:S(2)}) %all-to-all-start.1) | async-done | bytes 12320 | tf_op jit(solution)/shard_map/all_to_all | solution.py:19
  58.7 0.2 exponential_reduce_fusion
  58.9 0.6 broadcast_in_dim.40
  59.5 4.1 %all-to-all-start.2 = ((f32[32,1,96]{2,1,0:T(1,128)}), f32[32,1,96]{2,1,0:T(1,128)S(1)}, u32[]{:S(2)}, u32[]{:S(2)}) async-start(f32[32,1,96]{2,1,0:T(1,128)} %broadcast_in_dim.40), calls=%async_computation.2 | async-start | bytes 32768 | tf_op jit(solution)/shard_map/all_to_all | solution.py:19
  63.7 0.0 reduce-scatter.2.cloned.1.call-start
  63.7 0.1 broadcast_in_dim.42
  63.8 0.0 copy-done.1
  63.9 0.1 sub.63
  63.9 0.1 sub.64
  64.0 6.6 %all-to-all-done.2 = f32[32,1,96]{2,1,0:T(1,128)S(1)} async-done(((f32[32,1,96]{2,1,0:T(1,128)}), f32[32,1,96]{2,1,0:T(1,128)S(1)}, u32[]{:S(2)}, u32[]{:S(2)}) %all-to-all-start.2) | async-done | bytes 12320 | tf_op jit(solution)/shard_map/all_to_all | solution.py:19
  70.7 0.0 copy-start.2
  70.7 0.1 sub.60
  70.8 0.1 sub.61
  70.9 14.0 %fusion.2 = f32[2048,2048]{1,0:T(8,128)} fusion(f32[768,2048]{1,0:T(8,128)} %get-tuple-element.13, f32[768]{0:T(1024)S(1)} %select_add_fusion, f32[2048]{0:T(1024)S(1)} %copy-done.3, bf16[96,8,2048]{2,1,0:T(8,128)(2,1)S(1)} %copy-done, f32[96,8]{1,0:T(8,128)S(1)} %copy.21, f32[96,2048]{1,0:T(8,128)} %copy.19), kind=kOutput, calls=%fused_computation.10 | convolution fusion | flops 6464471040 | bytes 27015168 | tf_op jit(solution)/shard_map/dot_general | solution.py:95
  84.9 0.0 reduce-scatter.2.cloned.1.call-update
  84.9 172.8 %reduce-scatter.2.cloned.1.call-done = f32[256,2048]{1,0:T(8,128)} async-done(((f32[2048,2048]{1,0:T(8,128)}), f32[256,2048]{1,0:T(8,128)}) %reduce-scatter.2.cloned.1.call-update) | async-done | bytes 2097168 | tf_op jit(solution)/shard_map/reduce_scatter | solution.py:94
  257.7 7.6 %all-to-all-start.3 = ((f32[32,8,2048]{2,1,0:T(8,128)}), f32[32,8,2048]{2,1,0:T(8,128)}, u32[]{:S(2)}, u32[]{:S(2)}) async-start(f32[32,8,2048]{2,1,0:T(8,128)} %bitcast.18), calls=%async_computation.4 | async-start | bytes 4194304 | tf_op jit(solution)/shard_map/all_to_all | solution.py:51
  265.4 0.0 copy-done.2
  265.4 0.7 fusion.8
  266.1 4.6 %multiply_reduce_fusion = f32[2048]{0:T(1024)S(1)} fusion(f32[768]{0:T(1024)S(1)} %select_add_fusion, f32[96,8]{1,0:T(8,128)S(1)} %copy.21, bf16[96,8,2048]{2,1,0:T(8,128)(2,1)S(1)} %copy-done, f32[96,2048]{1,0:T(8,128)} %copy.19, f32[768,2048]{1,0:T(8,128)} %get-tuple-element.13), kind=kLoop, calls=%fused_computation | loop fusion | flops 18872320 | bytes 10237952 | tf_op jit(solution)/shard_map/reduce_sum | solution.py:90
  270.7 14.5 %all-reduce = (f32[2048]{0:T(1024)S(1)}, f32[]{:T(128)}) all-reduce(f32[2048]{0:T(1024)S(1)} %multiply_reduce_fusion, f32[]{:T(128)} %fusion.8), channel_id=1, replica_groups=mesh['state'=8,'act_0'=4,'act_1'=4,'act_2'=2] {'state'}, use_global_device_ids=true, to_apply=%region_9.10 | all-reduce | flops 2049 | bytes 16392 | tf_op jit(solution)/shard_map/psum | solution.py:56
  285.2 10.1 %all-reduce.2 = (f32[2048]{0:T(1024)S(1)}, f32[]{:T(128)}) all-reduce(f32[2048]{0:T(1024)S(1)} %get-tuple-element.4, f32[]{:T(128)} %get-tuple-element.5), channel_id=1, replica_groups=mesh['state'=8,'act_0'=4,'act_1'=4,'act_2'=2] {'act_0'}, use_global_device_ids=true, to_apply=%region_10.11 | all-reduce | flops 2049 | bytes 16392 | tf_op jit(solution)/shard_map/psum | solution.py:56
  295.3 9.0 %all-reduce.1 = (f32[2048]{0:T(1024)S(1)}, f32[]{:T(128)}) all-reduce(f32[2048]{0:T(1024)S(1)} %get-tuple-element.8, f32[]{:T(128)} %get-tuple-element.9), channel_id=1, replica_groups=mesh['state'=8,'act_0'=4,'act_1'=4,'act_2'=2] {'act_1'}, use_global_device_ids=true, to_apply=%region_11.12 | all-reduce | flops 2049 | bytes 16392 | tf_op jit(solution)/shard_map/psum | solution.py:56
  304.3 9.0 %all-reduce.3 = (f32[2048]{0:T(1024)}, f32[]{:T(128)}) all-reduce(f32[2048]{0:T(1024)S(1)} %get-tuple-element.6, f32[]{:T(128)} %get-tuple-element.7), channel_id=1, replica_groups=mesh['state'=8,'act_0'=4,'act_1'=4,'act_2'=2] {'act_2'}, use_global_device_ids=true, to_apply=%region_12.13 | all-reduce | flops 2049 | bytes 16392 | tf_op jit(solution)/shard_map/psum | solution.py:56
  314.0 0.0 all-to-all-done.3
  314.0 2.3 reduce_sum.67
  (7 shorter events, 0.1 us)
Async XLA Ops:
  7.2 24.6 %copy-start = (bf16[96,8,2048]{2,1,0:T(8,128)(2,1)S(1)}, bf16[96,8,2048]{2,1,0:T(8,128)(2,1)}, u32[]{:S(2)}) copy-start(bf16[96,8,2048]{2,1,0:T(8,128)(2,1)} %param.6) | copy-start | bytes 9437188
  7.2 26.8 %copy-start.3 = (f32[2048]{0:T(1024)S(1)}, f32[2048]{0:T(1024)}, u32[]{:S(2)}) copy-start(f32[2048]{0:T(1024)} %param.9) | copy-start | bytes 24580
  33.9 29.9 %copy-start.1 = (f32[96]{0:T(128)S(1)}, f32[96]{0:T(128)}, u32[]{:S(2)}) copy-start(f32[96]{0:T(128)} %param.7) | copy-start | bytes 1156
  48.2 10.5 %all-to-all-start.1 = ((f32[32,1,96]{2,1,0:T(1,128)}), f32[32,1,96]{2,1,0:T(1,128)S(1)}, u32[]{:S(2)}, u32[]{:S(2)}) async-start(f32[32,1,96]{2,1,0:T(1,128)} %broadcast_in_dim.39), calls=%async_computation.1 | async-start | bytes 32768 | tf_op jit(solution)/shard_map/all_to_all | solution.py:19
  59.5 11.2 %all-to-all-start.2 = ((f32[32,1,96]{2,1,0:T(1,128)}), f32[32,1,96]{2,1,0:T(1,128)S(1)}, u32[]{:S(2)}, u32[]{:S(2)}) async-start(f32[32,1,96]{2,1,0:T(1,128)} %broadcast_in_dim.40), calls=%async_computation.2 | async-start | bytes 32768 | tf_op jit(solution)/shard_map/all_to_all | solution.py:19
  63.7 194.1 %reduce-scatter.2.cloned.1.call-start = ((), (), s32[]{:S(2)}) async-start(), calls=%async_computation.5 | async-start | bytes 18874368 | tf_op jit(solution)/shard_map/reduce_scatter | solution.py:94
  70.7 194.7 %copy-start.2 = (f32[96]{0:T(128)}, f32[96]{0:T(128)S(1)}, u32[]{:S(2)}) copy-start(f32[96]{0:T(128)S(1)} %log_add_fusion) | copy-start | bytes 1156
  257.7 56.2 %all-to-all-start.3 = ((f32[32,8,2048]{2,1,0:T(8,128)}), f32[32,8,2048]{2,1,0:T(8,128)}, u32[]{:S(2)}, u32[]{:S(2)}) async-start(f32[32,8,2048]{2,1,0:T(8,128)} %bitcast.18), calls=%async_computation.4 | async-start | bytes 4194304 | tf_op jit(solution)/shard_map/all_to_all | solution.py:51
Sparse Core Ops, SparseCore 0:
  85.1 172.6 reduce-scatter.1
where the time goes:
time: 325 us; the launch traced here: 324 us
  waiting for transfers between devices  186 us (57%)
  blocking collectives  62.6 us (19%)
  matrix products  27.4 us (8%)
  between operations  16 us (5%)
  starting transfers between devices  15.4 us (5%)
  other arithmetic  11.1 us (3%)
  local copies, waits for them, and re-layouts  5.41 us (2%)
    reduce_scatter x1, waiting for transfers between devices, body(): lax.psum_scatter(lax.dot_general(flat_rows, back_grad, (((0,), (0,)), (()...  173 us
    psum x4, blocking collectives, over_axes(): return functools.reduce(lax.psum, axes, value)  42.7 us
    all_to_all x1, blocking collectives, sent_to_all(): return lax.all_to_all(copies, axis, split_axis=0, concat_axis=0, tiled=True)  20 us
    dot_general x1, matrix products, body(): lax.dot_general(flat_rows, back_grad, (((0,), (0,)), ((), ())), preferred...  14 us
    all_to_all x2, waiting for transfers between devices, sent_to_all(): return lax.all_to_all(copies, axis, split_axis=0, concat_axis=0, tiled=True)  13.5 us
    dot_general x1, matrix products, body(): preact = jnp.dot(flat_rows, w_hidden, preferred_element_type=jnp.float32)  13.4 us
    all_to_all x2, starting transfers between devices, sent_to_all(): return lax.all_to_all(copies, axis, split_axis=0, concat_axis=0, tiled=True)  7.76 us
    all_to_all x1, starting transfers between devices, sum_at_owner(): parts = lax.all_to_all(split_up(value, dim, count), axis, 0, 0, tiled=True)  7.64 us
  transfers between devices with their start and end apart: 4, of which 3 were waited for; matrix products, arithmetic and copies ran while one was open for 2% of the time, Pallas kernels for 0%

commit v1 on v0

v1 whole, which is shorter than its diff:
```python
import jax
import jax.numpy as jnp
from jax import lax
from jax.experimental import pallas as pl
from jax.experimental.pallas import tpu as pltpu
from jax.sharding import Mesh
from jax.sharding import PartitionSpec as P

Z, X, Y, C = "state", "act_0", "act_1", "act_2"
ACT = (X, Y, C)
STATE_ACT = (Z, X, Y, C)

norm_epsilon = 1e-06
penalty_weight = 2.0

F32 = jnp.float32
BF16 = jnp.bfloat16
STATES = 96
ACTIONS = 8
ROWS = STATES * ACTIONS
WIDTH = 2048
HALF = WIDTH // 2
CHUNK = 256
SUB = 32
AHEAD = 384
LAST = 256
VECTOR = HALF + 128


def remote(src, dst, send, recv, **target):
    return pltpu.make_async_remote_copy(
        src_ref=src,
        dst_ref=dst,
        send_sem=send,
        recv_sem=recv,
        device_id=target,
        device_id_type=pl.DeviceIdType.MESH,
    )


def kernel(
    state_ref,
    act_hbm,
    targets_ref,
    w_hbm,
    head_ref,
    grad_ref,
    grad_head_ref,
    lse_ref,
    loss_ref,
    w_buf,
    act_buf,
    state_pair,
    state_all,
    state_f32,
    normed,
    preact,
    head_in,
    slope,
    back,
    score_part,
    score_peer,
    score_grad,
    lse_all,
    vec_x,
    vec_y,
    vec_z,
    vec_c,
    gx,
    gy,
    gz,
    far_x,
    far_y,
    near_x,
    near_y,
    mid_x,
    mid_y,
    last_x,
    last_y,
    far_z,
    near_z,
    mid_z,
    last_z,
    total,
    total_peer,
    sem_in,
    pair_sem,
    state_sem,
    rows_sem,
    score_sem,
    lse_sem,
    vec_x_sem,
    vec_y_sem,
    vec_z_sem,
    vec_c_sem,
    far_sem,
    near_sem,
    mid_sem,
    last_sem,
    far_z_sem,
    near_z_sem,
    mid_z_sem,
    last_z_sem,
    total_sem,
):
    z, x, y, c = (lax.axis_index(name) for name in (Z, X, Y, C))
    other = 1 - c
    half = pl.ds(pl.multiple_of(c * HALF, HALF), HALF)
    other_half = pl.ds(pl.multiple_of(other * HALF, HALF), HALF)

    def at(axis, step):
        if axis == Z:
            return lax.rem(z + step + 8, 8)
        return lax.rem((x if axis == X else y) + step + 4, 4)

    act_in = [
        pltpu.make_async_copy(
            act_hbm.at[pl.ds(i * CHUNK, CHUNK)], act_buf.at[pl.ds(i * CHUNK, CHUNK)], sem_in.at[i]
        )
        for i in range(3)
    ]
    w_in = pltpu.make_async_copy(w_hbm.at[:, half], w_buf, sem_in.at[3])
    for copy in act_in:
        copy.start()
    w_in.start()

    barrier = pltpu.get_barrier_semaphore()
    plane = [(dx, dy) for dx in range(4) for dy in range(4) if dx or dy]

    def greet(**target):
        pl.semaphore_signal(barrier, inc=1, device_id=target, device_id_type=pl.DeviceIdType.MESH)

    greet(**{C: other})
    for dx, dy in plane:
        greet(**{X: at(X, dx), Y: at(Y, dy)})
    for dz in range(1, 8):
        greet(**{Z: at(Z, dz)})
    pl.semaphore_wait(barrier, 1 + len(plane) + 7)

    pair = remote(state_ref, state_pair, pair_sem.at[0], pair_sem.at[1], **{C: other})
    pair.start()
    pair.wait_recv()
    mine, theirs = state_ref[...].astype(F32), state_pair[...].astype(F32)
    low = jnp.where(c == 0, mine, theirs)
    high = jnp.where(c == 0, theirs, mine)
    state_all[0] = jnp.concatenate([low, high], axis=1).astype(BF16)
    state_out = [
        remote(
            state_all.at[0],
            state_all.at[dx * 4 + dy],
            state_sem.at[0, dx * 4 + dy],
            state_sem.at[1, dx * 4 + dy],
            **{X: at(X, dx), Y: at(Y, dy)},
        )
        for dx, dy in plane
    ]
    for copy in state_out:
        copy.start()
    for copy in state_out:
        copy.wait_recv()
    for j in range(16):
        slot = lax.rem(x - j // 4 + 4, 4) * 4 + lax.rem(y - j % 4 + 4, 4)
        state_f32[:, j * 128 : (j + 1) * 128] = state_all[slot].astype(F32)

    def rows_out(i):
        return remote(
            normed.at[pl.ds(i * CHUNK, CHUNK)],
            normed.at[pl.ds(ROWS + i * CHUNK, CHUNK)],
            rows_sem.at[0, i],
            rows_sem.at[1, i],
            **{C: other},
        )

    def normalise(t, carry):
        first = pl.multiple_of(t * 16, 16)
        pieces = [
            jnp.broadcast_to(state_f32[pl.ds(2 * t + i, 1), :], (8, WIDTH)) for i in range(2)
        ]
        mixture = jnp.concatenate(pieces, 0) + act_buf[pl.ds(first, 16), :].astype(F32)
        scale = lax.rsqrt(jnp.mean(mixture * mixture, -1, keepdims=True) + norm_epsilon)
        normed[pl.ds(first, 16), :] = (mixture * scale).astype(BF16)
        return carry

    for i in range(3):
        act_in[i].wait()
        lax.fori_loop(i * 16, (i + 1) * 16, normalise, 0, unroll=2)
        rows_out(i).start()

    lane8 = lax.broadcasted_iota(jnp.int32, (8, 128), 1)
    row8 = lax.broadcasted_iota(jnp.int32, (8, 128), 0)

    def pick(core):
        return (lane8 == row8 + core * 8)[None]

    def hidden(i, carry):
        base = pl.multiple_of(i * CHUNK, CHUNK)
        preact[...] = jnp.dot(
            normed[pl.ds(base, CHUNK), :], w_buf[...], preferred_element_type=F32
        )
        core = jnp.where(i < 3, c, other)
        mask = pick(core)

        def finish(t, inner):
            sub = pl.ds(pl.multiple_of(t * SUB, SUB), SUB)
            rows = pl.ds(pl.multiple_of(base + t * SUB, SUB), SUB)
            p = preact[sub, :]
            w = head_ref[:, half]
            g = jax.nn.sigmoid(p)
            pg = p * g
            h = normed[rows, half].astype(F32) + pg
            head_in[rows, :] = h
            slope[rows, :] = w * (g + pg * (1.0 - g))
            s = jnp.sum(h * w, -1, keepdims=True).reshape(SUB // 8, 8, 1)
            score_part[pl.ds(i * (CHUNK // 8) + t * (SUB // 8), SUB // 8), :] = jnp.sum(
                jnp.where(mask, s, 0.0), 1
            )
            return inner

        lax.fori_loop(0, CHUNK // SUB, finish, 0)
        return carry

    w_in.wait()
    lax.fori_loop(0, 3, hidden, 0)

    def hidden_peer(i, carry):
        rows_out(i - 3).wait_recv()
        return hidden(i, carry)

    lax.fori_loop(3, 6, hidden_peer, 0)

    score_part[pl.ds(0, STATES), :] = score_part[pl.ds(0, STATES), :] + score_part[
        pl.ds(STATES, STATES), :
    ]
    scores_out = remote(
        score_part.at[pl.ds(0, STATES)], score_peer, score_sem.at[0], score_sem.at[1], **{C: other}
    )
    scores_out.start()
    scores_out.wait_recv()
    scores = score_part[pl.ds(0, STATES), :] + score_peer[...]
    lane = lax.broadcasted_iota(jnp.int32, (STATES, 128), 1)
    row = lax.broadcasted_iota(jnp.int32, (STATES, 128), 0)
    valid = lane < 16
    eye = lane == row
    top = jnp.max(jnp.where(valid, scores, -jnp.inf), -1, keepdims=True)
    local = jnp.sum(jnp.where(valid, jnp.exp(scores - top), 0.0), -1, keepdims=True)
    lse_all[0] = jnp.sum(jnp.where(eye, top + jnp.log(local), 0.0), 0, keepdims=True)
    lse_out = [
        remote(
            lse_all.at[0],
            lse_all.at[dx * 4 + dy],
            lse_sem.at[0, dx * 4 + dy],
            lse_sem.at[1, dx * 4 + dy],
            **{X: at(X, dx), Y: at(Y, dy)},
        )
        for dx, dy in plane
    ]
    for copy in lse_out:
        copy.start()
    for copy in lse_out:
        copy.wait_recv()
    parts = [
        lse_all[lax.rem(x - j // 4 + 4, 4) * 4 + lax.rem(y - j % 4 + 4, 4)] for j in range(16)
    ]
    peak = parts[0]
    for part in parts[1:]:
        peak = jnp.maximum(peak, part)
    mass = jnp.exp(parts[0] - peak)
    for part in parts[1:]:
        mass = mass + jnp.exp(part - peak)
    lse_row = peak + jnp.log(mass)
    lse_ref[...] = lse_row[:, :STATES]
    lse = jnp.sum(jnp.where(eye, lse_row, 0.0), -1, keepdims=True)
    eye_states = lax.broadcasted_iota(jnp.int32, (STATES, STATES), 1) == lax.broadcasted_iota(
        jnp.int32, (STATES, STATES), 0
    )
    target = jnp.sum(jnp.where(eye_states, targets_ref[...], 0.0), -1, keepdims=True)
    data_lane = jnp.where((x == 0) & (y == 0), 0, -1)
    is_data = lane == data_lane
    gap = scores - target
    score_grad[...] = jnp.where(
        valid, penalty_weight * jnp.exp(scores - lse), 0.0
    ) + jnp.where(is_data, gap - penalty_weight, 0.0)
    loss_terms = jnp.where(is_data, penalty_weight * (lse - scores) + 0.5 * gap * gap, 0.0)
    loss_here = jnp.sum(jnp.sum(loss_terms, 0, keepdims=True), -1, keepdims=True)
    loss_here = jnp.where(c == 0, loss_here, 0.0)

    def backward(t, head_sum):
        rows = pl.ds(pl.multiple_of(t * SUB, SUB), SUB)
        own = t < ROWS // SUB
        core = jnp.where(own, c, other)
        states = pl.multiple_of((t - jnp.where(own, 0, ROWS // SUB)) * (SUB // 8), SUB // 8)
        pieces = []
        for i in range(SUB // 8):
            line = jnp.broadcast_to(score_grad[pl.ds(states + i, 1), :], (8, 128))
            pieces.append(
                jnp.sum(jnp.where(lane8 == row8 + core * 8, line, 0.0), -1, keepdims=True)
            )
        g = jnp.concatenate(pieces, 0)
        back[rows, :] = (g * slope[rows, :]).astype(BF16)
        return head_sum + jnp.sum((g * head_in[rows, :]).reshape(SUB // 8, 8, HALF), 0)

    head_sum = lax.fori_loop(
        0, 2 * ROWS // SUB, backward, jnp.zeros((8, HALF), F32), unroll=1
    )
    vec_x[0, :, :HALF] = jnp.sum(head_sum, 0, keepdims=True)
    vec_x[0, :, HALF:] = jnp.broadcast_to(loss_here, (1, 128))

    def vec_copies(axis, buf, sem, count):
        return [
            remote(buf.at[0], buf.at[d], sem.at[0, d], sem.at[1, d], **{axis: at(axis, d)})
            for d in range(1, count)
        ]

    def vec_sum(buf, me, count):
        result = buf[me]
        for q in range(1, count):
            result = result + buf[lax.rem(me - q + count, count)]
        return result

    vec_x_out = vec_copies(X, vec_x, vec_x_sem, 4)
    vec_y_out = vec_copies(Y, vec_y, vec_y_sem, 4)
    vec_z_out = vec_copies(Z, vec_z, vec_z_sem, 8)
    vec_c_out = remote(vec_c.at[0], vec_c.at[1], vec_c_sem.at[0], vec_c_sem.at[1], **{C: other})
    for copy in vec_x_out:
        copy.start()

    def vec_step_y():
        for copy in vec_x_out:
            copy.wait_recv()
        vec_y[0] = vec_sum(vec_x, x, 4)
        for copy in vec_y_out:
            copy.start()

    def vec_step_z():
        for copy in vec_y_out:
            copy.wait_recv()
        vec_z[0] = vec_sum(vec_y, y, 4)
        for copy in vec_z_out:
            copy.start()

    def vec_step_c():
        for copy in vec_z_out:
            copy.wait_recv()
        vec_c[0] = vec_sum(vec_z, z, 8)
        vec_c_out.start()

    def target_z(k):
        return lax.rem(z + jnp.where(lax.rem(k, 2) == 1, 4 - (k + 1) // 2, 4 + k // 2), 8)

    branches = (
        (0, X, Y, x, y, gx, far_x, near_x, mid_x, last_x),
        (1, Y, X, y, x, gy, far_y, near_y, mid_y, last_y),
    )

    def far_copies(k, b):
        i, axis, _, me, _, g, far, _, _, _ = branches[b]
        zz = target_z(k)
        opposite = at(axis, 2)
        return [
            remote(
                g.at[zz, opposite, pl.ds(2 * s, 2)],
                far.at[k, s],
                far_sem.at[0, i, k, s],
                far_sem.at[1, i, k, s],
                **{axis: at(axis, 1 - 2 * s)},
            )
            for s in range(2)
        ]

    def near_copies(k, b):
        i, axis, _, me, _, g, _, near, _, _ = branches[b]
        zz = target_z(k)
        return [
            remote(
                g.at[zz, at(axis, 1 - 2 * s)],
                near.at[k, s],
                near_sem.at[0, i, k, s],
                near_sem.at[1, i, k, s],
                **{axis: at(axis, 1 - 2 * s)},
            )
            for s in range(2)
        ]

    def mid_copies(k, b):
        i, _, axis, me, _, g, _, _, mid, _ = branches[b]
        zz = target_z(k)
        return [
            remote(
                g.at[zz, me, at(axis, d)],
                mid.at[k, d - 1],
                mid_sem.at[0, i, k, d - 1],
                mid_sem.at[1, i, k, d - 1],
                **{axis: at(axis, d)},
            )
            for d in range(1, 4)
        ]

    def last_copy(k, b):
        i, _, _, me, me2, g, _, _, _, last = branches[b]
        zz = target_z(k)
        return remote(
            g.at[zz, me, me2],
            last.at[k],
            last_sem.at[0, i, k],
            last_sem.at[1, i, k],
            **{Z: zz},
        )

    def block(k):
        zz = target_z(k)
        columns = pl.ds(pl.multiple_of(zz * 256, 256), 256)
        product = lax.dot_general(
            normed[:, columns],
            back[...],
            (((0,), (0,)), ((), ())),
            preferred_element_type=F32,
        ).astype(BF16)
        for i in range(4):
            for j in range(4):
                part = product[i * 64 + j * 16 : i * 64 + j * 16 + 16, :]
                gx[zz, i, j] = part[:, :AHEAD]
                gy[zz, j, i] = part[:, AHEAD : 2 * AHEAD]
                gz[zz, i, j] = part[:, 2 * AHEAD :]
        for b in range(2):
            for copy in far_copies(k, b):
                copy.start()

    def stage_near(k):
        zz = target_z(k)
        for b in range(2):
            _, axis, _, _, _, g, far, _, _, _ = branches[b]
            for s, arrived in enumerate(far_copies(k, b)):
                arrived.wait_recv()
                slot = at(axis, 1 - 2 * s)
                ref = g.at[zz, slot, pl.ds(2 * s, 2)]
                ref[...] = (ref[...].astype(F32) + far[k, s].astype(F32)).astype(BF16)
            for copy in near_copies(k, b):
                copy.start()

    def stage_mid(k):
        zz = target_z(k)
        for b in range(2):
            _, _, _, me, _, g, _, near, _, _ = branches[b]
            for copy in near_copies(k, b):
                copy.wait_recv()
            g[zz, me] = (
                g[zz, me].astype(F32) + near[k, 0].astype(F32) + near[k, 1].astype(F32)
            ).astype(BF16)
            for copy in mid_copies(k, b):
                copy.start()

    def mid_total(k, b):
        _, _, _, me, me2, g, _, _, mid, _ = branches[b]
        for copy in mid_copies(k, b):
            copy.wait_recv()
        result = g[target_z(k), me, me2].astype(F32)
        for d in range(3):
            result = result + mid[k, d].astype(F32)
        return result

    def stage_last(k):
        zz = target_z(k)
        for b in range(2):
            _, _, _, me, me2, g, _, _, _, _ = branches[b]
            g[zz, me, me2] = mid_total(k, b).astype(BF16)
            last_copy(k, b).start()

    far_z_out = [
        remote(
            gz.at[at(Z, 4), pl.ds(2 * s, 2)],
            far_z.at[s],
            far_z_sem.at[0, s],
            far_z_sem.at[1, s],
            **{Z: at(Z, 1 - 2 * s)},
        )
        for s in range(2)
    ]

    def near_z_copy(j, s):
        return remote(
            gz.at[at(Z, j * (1 - 2 * s))],
            near_z.at[s, j - 1],
            near_z_sem.at[0, s, j - 1],
            near_z_sem.at[1, s, j - 1],
            **{Z: at(Z, 1 - 2 * s)},
        )

    def stage_z(j):
        for s in range(2):
            slot = at(Z, j * (1 - 2 * s))
            if j == 3:
                far_z_out[s].wait_recv()
                ref = gz.at[slot, pl.ds(2 * s, 2)]
                ref[...] = (ref[...].astype(F32) + far_z[s].astype(F32)).astype(BF16)
            else:
                near_z_copy(j + 1, s).wait_recv()
                gz[slot] = (gz[slot].astype(F32) + near_z[s, j].astype(F32)).astype(BF16)
            near_z_copy(j, s).start()

    mid_z_out = [
        remote(
            gz.at[z, at(X, d)],
            mid_z.at[d - 1],
            mid_z_sem.at[0, d - 1],
            mid_z_sem.at[1, d - 1],
            **{X: at(X, d)},
        )
        for d in range(1, 4)
    ]
    last_z_out = [
        remote(
            gz.at[z, x, at(Y, d)],
            last_z.at[d - 1],
            last_z_sem.at[0, d - 1],
            last_z_sem.at[1, d - 1],
            **{Y: at(Y, d)},
        )
        for d in range(1, 4)
    ]

    def stage_z_mid():
        for s in range(2):
            near_z_copy(1, s).wait_recv()
        gz[z] = (
            gz[z].astype(F32) + near_z[0, 0].astype(F32) + near_z[1, 0].astype(F32)
        ).astype(BF16)
        for copy in mid_z_out:
            copy.start()

    def stage_z_last():
        for copy in mid_z_out:
            copy.wait_recv()
        sums = gz[z, x].astype(F32)
        for d in range(3):
            sums = sums + mid_z[d].astype(F32)
        gz[z, x] = sums.astype(BF16)
        for copy in last_z_out:
            copy.start()

    def step(t, carry):
        @pl.when(t < 8)
        def _():
            block(t)

        @pl.when(t == 0)
        def _():
            for copy in far_z_out:
                copy.start()

        for when, j in ((3, 3), (6, 2), (8, 1)):

            @pl.when(t == when)
            def _(j=j):
                stage_z(j)

        @pl.when((t >= 2) & (t < 10))
        def _():
            stage_near(t - 2)

        @pl.when((t >= 4) & (t < 12))
        def _():
            stage_mid(t - 4)

        @pl.when((t >= 6) & (t < 13))
        def _():
            stage_last(t - 6)

        for when, part in (
            (2, vec_step_y),
            (5, vec_step_z),
            (7, vec_step_c),
            (10, stage_z_mid),
            (12, stage_z_last),
        ):

            @pl.when(t == when)
            def _(part=part):
                part()

        return carry

    lax.fori_loop(0, 13, step, 0)

    for b in range(2):
        last = branches[b][9]
        result = mid_total(7, b)
        for k in range(7):
            last_copy(k, b).wait_recv()
            result = result + last[k].astype(F32)
        for i in range(2):
            total[i, :, b * AHEAD : (b + 1) * AHEAD] = result[8 * i : 8 * i + 8, :]
    for copy in last_z_out:
        copy.wait_recv()
    result = gz[z, x, y].astype(F32)
    for d in range(3):
        result = result + last_z[d].astype(F32)
    for i in range(2):
        total[i, :, 2 * AHEAD :] = result[8 * i : 8 * i + 8, :]
    total_out = remote(
        total.at[other], total_peer, total_sem.at[0], total_sem.at[1], **{C: other}
    )
    total_out.start()

    vec_c_out.wait_recv()
    grad_head_ref[:, half] = vec_c[0, :, :HALF]
    grad_head_ref[:, other_half] = vec_c[1, :, :HALF]
    loss_ref[...] = (vec_c[0, :, HALF:] + vec_c[1, :, HALF:]) * (1.0 / (STATES * 8))
    grad_ref[:, half] = total[c]

    sent = [pair, scores_out, vec_c_out]
    sent += state_out + lse_out + vec_x_out + vec_y_out + vec_z_out
    sent += far_z_out + mid_z_out + last_z_out
    sent += [rows_out(i) for i in range(3)]
    sent += [near_z_copy(j, s) for j in range(1, 4) for s in range(2)]
    for copy in sent:
        copy.wait_send()

    def drain(k, carry):
        for b in range(2):
            for copy in far_copies(k, b) + near_copies(k, b) + mid_copies(k, b):
                copy.wait_send()

            @pl.when(k < 7)
            def _(b=b):
                last_copy(k, b).wait_send()

        return carry

    lax.fori_loop(0, 8, drain, 0)
    total_out.wait()
    grad_ref[:, other_half] = total_peer[...]


def body(state_features, action_features, targets, w_hidden, w_head):
    vmem = pl.BlockSpec(memory_space=pltpu.VMEM)
    anywhere = pl.BlockSpec(memory_space=pl.ANY)
    dma = pltpu.SemaphoreType.DMA
    scratch = [
        pltpu.VMEM((WIDTH, HALF), BF16),
        pltpu.VMEM((ROWS, WIDTH), BF16),
        pltpu.VMEM((STATES, 64), BF16),
        pltpu.VMEM((16, STATES, 128), BF16),
        pltpu.VMEM((STATES, WIDTH), F32),
        pltpu.VMEM((2 * ROWS, WIDTH), BF16),
        pltpu.VMEM((CHUNK, HALF), F32),
        pltpu.VMEM((2 * ROWS, HALF), F32),
        pltpu.VMEM((2 * ROWS, HALF), F32),
        pltpu.VMEM((2 * ROWS, HALF), BF16),
        pltpu.VMEM((2 * STATES, 128), F32),
        pltpu.VMEM((STATES, 128), F32),
        pltpu.VMEM((STATES, 128), F32),
        pltpu.VMEM((16, 1, 128), F32),
        pltpu.VMEM((4, 1, VECTOR), F32),
        pltpu.VMEM((4, 1, VECTOR), F32),
        pltpu.VMEM((8, 1, VECTOR), F32),
        pltpu.VMEM((2, 1, VECTOR), F32),
        pltpu.VMEM((8, 4, 4, 16, AHEAD), BF16),
        pltpu.VMEM((8, 4, 4, 16, AHEAD), BF16),
        pltpu.VMEM((8, 4, 4, 16, LAST), BF16),
        pltpu.VMEM((8, 2, 2, 16, AHEAD), BF16),
        pltpu.VMEM((8, 2, 2, 16, AHEAD), BF16),
        pltpu.VMEM((8, 2, 4, 16, AHEAD), BF16),
        pltpu.VMEM((8, 2, 4, 16, AHEAD), BF16),
        pltpu.VMEM((8, 3, 16, AHEAD), BF16),
        pltpu.VMEM((8, 3, 16, AHEAD), BF16),
        pltpu.VMEM((8, 16, AHEAD), BF16),
        pltpu.VMEM((8, 16, AHEAD), BF16),
        pltpu.VMEM((2, 2, 4, 16, LAST), BF16),
        pltpu.VMEM((2, 3, 4, 4, 16, LAST), BF16),
        pltpu.VMEM((3, 4, 16, LAST), BF16),
        pltpu.VMEM((3, 16, LAST), BF16),
        pltpu.VMEM((2, 8, HALF), F32),
        pltpu.VMEM((8, HALF), F32),
        dma((4,)),
        dma((2,)),
        dma((2, 16)),
        dma((2, 3)),
        dma((2,)),
        dma((2, 16)),
        dma((2, 4)),
        dma((2, 4)),
        dma((2, 8)),
        dma((2,)),
        dma((2, 2, 8, 2)),
        dma((2, 2, 8, 2)),
        dma((2, 2, 8, 3)),
        dma((2, 2, 8)),
        dma((2, 2)),
        dma((2, 2, 3)),
        dma((2, 3)),
        dma((2, 3)),
        dma((2,)),
    ]
    grad, grad_head, lse, loss = pl.pallas_call(
        kernel,
        out_shape=(
            jax.ShapeDtypeStruct((8, WIDTH), F32),
            jax.ShapeDtypeStruct((1, WIDTH), F32),
            jax.ShapeDtypeStruct((1, STATES), F32),
            jax.ShapeDtypeStruct((1, 128), F32),
        ),
        in_specs=[vmem, anywhere, vmem, anywhere, vmem],
        out_specs=(vmem,) * 4,
        scratch_shapes=scratch,
        compiler_params=pltpu.CompilerParams(
            collective_id=0, has_side_effects=True, vmem_limit_bytes=62 * 1024 * 1024
        ),
        name="critic",
    )(
        state_features,
        action_features.reshape(ROWS, WIDTH),
        targets.reshape(1, STATES),
        w_hidden,
        w_head.reshape(1, WIDTH),
    )
    return grad, grad_head.reshape(WIDTH), lse.reshape(STATES), loss[0, 0]


def solution(mesh):
    finer = Mesh(mesh.devices.reshape(8, 4, 4, 2), (Z, X, Y, C))
    return jax.shard_map(
        body,
        mesh=finer,
        in_specs=(P(Z, ACT), P(Z, ACT, None), P(Z), P(), P()),
        out_specs=(P(STATE_ACT, None), P(), P(Z), P()),
        check_vma=False,
    )
```

time: 325 us -> 95.8 us (0.29)
  waiting for transfers between devices: 186 us -> 0 us
  Pallas kernels: 0 us -> 87.8 us
  blocking collectives: 62.6 us -> 0 us
  matrix products: 27.4 us -> 0 us
  starting transfers between devices: 15.4 us -> 0 us
  between operations: 16 us -> 2.46 us
  other arithmetic: 11.1 us -> 0 us
    reduce_scatter x1 -> x0, waiting for transfers between devices: 173 us -> none  [body(): lax.psum_scatter(lax.dot_general(flat_rows, back_grad, (((0,), (0,)), (()...]
    pallas_call x0 -> x1, Pallas kernels: none -> 87.8 us  [body(): pl.pallas_call(kernel, out_shape=(jax.ShapeDtypeStruct((8, WIDTH), F32),...]
    psum x4 -> x0, blocking collectives: 42.7 us -> none  [over_axes(): return functools.reduce(lax.psum, axes, value)]
    dot_general x2 -> x0, matrix products: 27.4 us -> none  [the longest x1 14 us: body(): lax.dot_general(flat_rows, back_grad, (((0,), (0,)), ((), ())), preferred...]
    all_to_all x1 -> x0, blocking collectives: 20 us -> none  [sent_to_all(): return lax.all_to_all(copies, axis, split_axis=0, concat_axis=0, tiled=True)]
    all_to_all x3 -> x0, starting transfers between devices: 15.4 us -> none  [the longest x2 7.76 us: sent_to_all(): return lax.all_to_all(copies, axis, split_axis=0, concat_axis=0, tiled=True)]
    all_to_all x3 -> x0, waiting for transfers between devices: 13.5 us -> none  [the longest x2 13.5 us: sent_to_all(): return lax.all_to_all(copies, axis, split_axis=0, concat_axis=0, tiled=True)]
    reduce_sum x6 -> x0, other arithmetic: 9.83 us -> none  [the longest x1 4.57 us: body(): head_local = jnp.sum(grad_flat[:, None] * head_input, 0)]
  transfers between devices with their start and end apart: 4 -> 0, of which waited for: 3 -> 0; matrix products, arithmetic and copies ran while one was open for 2% -> 0% of each run, Pallas kernels for 0% -> 0%
where the time goes in v1:
time: 95.8 us; the launch traced here: 95.5 us
  Pallas kernels  87.8 us (92%)
  local copies, waits for them, and re-layouts  5.29 us (6%)
  between operations  2.46 us (3%)
    pallas_call x1, Pallas kernels, body(): pl.pallas_call(kernel, out_shape=(jax.ShapeDtypeStruct((8, WIDTH), F32),...  87.8 us
    unnamed x4, local copies, waits for them, and re-layouts  5.29 us

profile of v1, /device:TPU:1, one launch (start us, length us, event | category | flops | bytes accessed | tf_op | source)
XLA Modules:
  0.0 95.5 jit_solution(18123393467015053915)
XLA Ops:
  0.6 1.4 %copy.9.state_ref = bf16[96,64]{1,0:T(8,128)(2,1)} copy(bf16[96,64]{0,1:T(8,128)(2,1)} %param.5) | data formatting | bytes 24576 | tf_op args[0]
  2.0 87.8 %critic.1 = (f32[8,2048]{1,0:T(8,128)}, f32[1,2048]{1,0:T(1,128)}, f32[1,96]{1,0:T(1,128)}, f32[1,128]{1,0:T(1,128)}) custom-call(bf16[96,64]{1,0:T(8,128)(2,1)} %copy.9.state_ref, bf16[768,2048]{1,0:T(8,128)(2,1)} %bitcast.7, f32[1,96]{1,0:T(1,128)} %bitcast.10, bf16[2048,2048]{1,0:T(8,128)(2,1)} %w_hbm.1, f32[1,2048]{1,0:T(1,128)} %bitcast.9), custom_call_target="tpu_custom_call" | custom-call | tf_op jit(solution)/shard_map/critic/pallas_call | solution.py:694
  89.8 1.5 %copy.14 = f32[8,2048]{1,0:T(8,128)} copy(f32[8,2048]{1,0:T(8,128)} %get-tuple-element.16) | data formatting | bytes 131072
  91.3 1.3 %copy.15 = f32[2048]{0:T(1024)} copy(f32[2048]{0:T(1024)} %bitcast.8) | data formatting | bytes 16384
  92.6 1.1 %copy.16 = f32[96]{0:T(128)} copy(f32[96]{0:T(128)} %bitcast.12) | data formatting | bytes 768

commit v2 on v1

v2 whole, which is shorter than its diff:
```python
import jax
import jax.numpy as jnp
from jax import lax
from jax.experimental import pallas as pl
from jax.experimental.pallas import tpu as pltpu
from jax.sharding import Mesh
from jax.sharding import PartitionSpec as P

Z, X, Y, C = "state", "act_0", "act_1", "act_2"
ACT = (X, Y, C)
STATE_ACT = (Z, X, Y, C)

norm_epsilon = 1e-06
penalty_weight = 2.0

F32 = jnp.float32
BF16 = jnp.bfloat16
STATES = 96
ACTIONS = 8
ROWS = STATES * ACTIONS
WIDTH = 2048
HALF = WIDTH // 2
CHUNK = 256
SUB = 32
AHEAD = 384
LAST = 256
VECTOR = HALF + 128
GROUPS = ((0,), (1, 2), (3, 4), (5, 6), (7,))
DEPTH = 2
PLUS = {4: 0, 3: 1, 2: 3, 1: 5}
MINUS = {3: 2, 2: 4, 1: 6}


def remote(src, dst, send, recv, **target):
    return pltpu.make_async_remote_copy(
        src_ref=src,
        dst_ref=dst,
        send_sem=send,
        recv_sem=recv,
        device_id=target,
        device_id_type=pl.DeviceIdType.MESH,
    )


def kernel(
    state_ref,
    act_hbm,
    targets_ref,
    w_hbm,
    head_ref,
    grad_ref,
    grad_head_ref,
    lse_ref,
    loss_ref,
    w_buf,
    act_buf,
    state_own,
    state_all,
    state_f32,
    normed,
    preact_a,
    preact_b,
    head_in,
    slope,
    back,
    score_lanes,
    score_part,
    score_peer,
    score_grad,
    grad_rows,
    lse_all,
    vec_x,
    vec_y,
    vec_z,
    vec_c,
    gx,
    gy,
    gz,
    far_x,
    far_y,
    near_x,
    near_y,
    mid_x,
    mid_y,
    last_x,
    last_y,
    far_z,
    near_z,
    plane_z,
    total,
    total_peer,
    sem_in,
    pair_sem,
    state_sem,
    rows_sem,
    score_sem,
    lse_sem,
    vec_x_sem,
    vec_y_sem,
    vec_z_sem,
    vec_c_sem,
    far_sem,
    near_sem,
    mid_sem,
    last_sem,
    far_z_sem,
    near_z_sem,
    plane_z_sem,
    total_sem,
):
    z, x, y, c = (lax.axis_index(name) for name in (Z, X, Y, C))
    other = 1 - c
    half = pl.ds(pl.multiple_of(c * HALF, HALF), HALF)
    other_half = pl.ds(pl.multiple_of(other * HALF, HALF), HALF)

    def at(axis, step):
        if axis == Z:
            return lax.rem(z + step + 8, 8)
        return lax.rem((x if axis == X else y) + step + 4, 4)

    act_in = [
        pltpu.make_async_copy(
            act_hbm.at[pl.ds(i * CHUNK, CHUNK)], act_buf.at[pl.ds(i * CHUNK, CHUNK)], sem_in.at[i]
        )
        for i in range(3)
    ]
    w_in = pltpu.make_async_copy(w_hbm.at[:, half], w_buf, sem_in.at[3])
    for copy in act_in:
        copy.start()
    w_in.start()

    barrier = pltpu.get_barrier_semaphore()
    plane = [(dx, dy) for dx in range(4) for dy in range(4) if dx or dy]

    def greet(**target):
        pl.semaphore_signal(barrier, inc=1, device_id=target, device_id_type=pl.DeviceIdType.MESH)

    greet(**{C: other})
    for dx, dy in plane:
        greet(**{X: at(X, dx), Y: at(Y, dy)})
    for dz in range(1, 8):
        greet(**{Z: at(Z, dz)})
    pl.semaphore_wait(barrier, 1 + len(plane) + 7)

    state_own[...] = jnp.zeros(state_own.shape, BF16)
    state_own[:, :STATES] = state_ref[...]
    state_all[c, 0] = state_own[...]
    state_out = [
        remote(
            state_own,
            state_all.at[c, dx * 4 + dy],
            state_sem.at[0, dx * 4 + dy],
            state_sem.at[1, dx * 4 + dy],
            **{X: at(X, dx), Y: at(Y, dy)},
        )
        for dx, dy in plane
    ]
    for copy in state_out:
        copy.start()
    for copy in state_out:
        copy.wait_recv()
    pair = remote(state_all.at[c], state_all.at[c], pair_sem.at[0], pair_sem.at[1], **{C: other})
    pair_in = remote(
        state_all.at[other], state_all.at[other], pair_sem.at[0], pair_sem.at[1], **{C: other}
    )
    pair.start()
    pair_in.wait_recv()
    for j in range(16):
        slot = lax.rem(x - j // 4 + 4, 4) * 4 + lax.rem(y - j % 4 + 4, 4)
        tile = jnp.concatenate([state_all[0, slot], state_all[1, slot]], 0).astype(F32)
        state_f32[:, j * 128 : (j + 1) * 128] = tile.T[:STATES, :]

    def rows_out(i):
        return remote(
            normed.at[pl.ds(i * CHUNK, CHUNK)],
            normed.at[pl.ds(ROWS + i * CHUNK, CHUNK)],
            rows_sem.at[0, i],
            rows_sem.at[1, i],
            **{C: other},
        )

    def mixture(u, j):
        tile = slice(j * 128, (j + 1) * 128)
        lines = state_f32[u * 8 : u * 8 + 8, tile]
        lines = jnp.broadcast_to(lines[:, None, :], (8, 8, 128)).reshape(64, 128)
        return lines + act_buf[u * 64 : u * 64 + 64, tile].astype(F32)

    def normalise(i):
        act_in[i].wait()
        for u in range(i * 4, i * 4 + 4):
            rows = slice(u * 64, u * 64 + 64)
            sums = None
            for j in range(WIDTH // 128):
                m = mixture(u, j)
                sums = m * m if sums is None else sums + m * m
            mean = jnp.sum(sums, -1, keepdims=True) * (1.0 / WIDTH)
            factor = jnp.broadcast_to(lax.rsqrt(mean + norm_epsilon), (64, 128))
            for j in range(WIDTH // 128):
                normed[rows, j * 128 : (j + 1) * 128] = (mixture(u, j) * factor).astype(BF16)

    lane8 = lax.broadcasted_iota(jnp.int32, (8, 128), 1)
    row8 = lax.broadcasted_iota(jnp.int32, (8, 128), 0)

    def product(i, buf):
        buf[...] = jnp.dot(
            normed[i * CHUNK : (i + 1) * CHUNK, :], w_buf[...], preferred_element_type=F32
        )

    def finish(i, buf):
        w = head_ref[:, half]
        for t in range(CHUNK // SUB):
            rows = slice(i * CHUNK + t * SUB, i * CHUNK + (t + 1) * SUB)
            p = buf[t * SUB : (t + 1) * SUB, :]
            g = 0.5 * jnp.tanh(0.5 * p) + 0.5
            pg = p * g
            h = normed[rows, half].astype(F32) + pg
            head_in[rows, :] = h
            slope[rows, :] = w * (g + pg * (1.0 - g))
            hw = h * w
            sums = hw[:, :128]
            for j in range(1, HALF // 128):
                sums = sums + hw[:, j * 128 : (j + 1) * 128]
            score_lanes[rows, :] = sums

    buffers = (preact_a, preact_b)
    normalise(0)
    rows_out(0).start()
    w_in.wait()
    for i in range(6):
        if i >= 3:
            rows_out(i - 3).wait_recv()
        product(i, buffers[i % 2])
        if i < 2:
            normalise(i + 1)
            rows_out(i + 1).start()
        if i > 0:
            finish(i - 1, buffers[(i - 1) % 2])
    finish(5, buffers[1])

    for i in range(3):
        states = 0.0
        for part, core in ((0, c), (1, other)):
            first = part * ROWS + i * CHUNK
            column = jnp.sum(score_lanes[first : first + CHUNK, :], -1, keepdims=True)
            column = column.reshape(CHUNK // 8, 8, 1)
            states = states + jnp.sum(
                jnp.where((lane8 == row8 + core * 8)[None], column, 0.0), 1
            )
        score_part[i * (CHUNK // 8) : (i + 1) * (CHUNK // 8), :] = states
    scores_out = remote(score_part, score_peer, score_sem.at[0], score_sem.at[1], **{C: other})
    scores_out.start()
    scores_out.wait_recv()
    scores = score_part[...] + score_peer[...]
    lane = lax.broadcasted_iota(jnp.int32, (STATES, 128), 1)
    row = lax.broadcasted_iota(jnp.int32, (STATES, 128), 0)
    valid = lane < 16
    eye = lane == row
    top = jnp.max(jnp.where(valid, scores, -jnp.inf), -1, keepdims=True)
    local = jnp.sum(jnp.where(valid, jnp.exp(scores - top), 0.0), -1, keepdims=True)
    lse_all[0] = jnp.sum(jnp.where(eye, top + jnp.log(local), 0.0), 0, keepdims=True)
    lse_out = [
        remote(
            lse_all.at[0],
            lse_all.at[dx * 4 + dy],
            lse_sem.at[0, dx * 4 + dy],
            lse_sem.at[1, dx * 4 + dy],
            **{X: at(X, dx), Y: at(Y, dy)},
        )
        for dx, dy in plane
    ]
    for copy in lse_out:
        copy.start()
    for copy in lse_out:
        copy.wait_recv()
    parts = [
        lse_all[lax.rem(x - j // 4 + 4, 4) * 4 + lax.rem(y - j % 4 + 4, 4)] for j in range(16)
    ]
    peak = parts[0]
    for part in parts[1:]:
        peak = jnp.maximum(peak, part)
    mass = jnp.exp(parts[0] - peak)
    for part in parts[1:]:
        mass = mass + jnp.exp(part - peak)
    lse_row = peak + jnp.log(mass)
    lse_ref[...] = lse_row[:, :STATES]
    lse = jnp.sum(jnp.where(eye, lse_row, 0.0), -1, keepdims=True)
    eye_states = lax.broadcasted_iota(jnp.int32, (STATES, STATES), 1) == lax.broadcasted_iota(
        jnp.int32, (STATES, STATES), 0
    )
    target = jnp.sum(jnp.where(eye_states, targets_ref[...], 0.0), -1, keepdims=True)
    data_lane = jnp.where((x == 0) & (y == 0), 0, -1)
    is_data = lane == data_lane
    gap = scores - target
    score_grad[...] = jnp.where(
        valid, penalty_weight * jnp.exp(scores - lse), 0.0
    ) + jnp.where(is_data, gap - penalty_weight, 0.0)
    loss_terms = jnp.where(is_data, penalty_weight * (lse - scores) + 0.5 * gap * gap, 0.0)
    loss_here = jnp.sum(jnp.sum(loss_terms, 0, keepdims=True), -1, keepdims=True)
    loss_here = jnp.where(c == 0, loss_here, 0.0)

    for part, core in ((0, c), (1, other)):
        for i in range(3):
            lines = score_grad[i * (CHUNK // 8) : (i + 1) * (CHUNK // 8), :]
            lines = jnp.broadcast_to(lines[:, None, :], (CHUNK // 8, 8, 128))
            lines = jnp.where((lane8 == row8 + core * 8)[None], lines, 0.0)
            column = jnp.sum(lines.reshape(CHUNK, 128), -1, keepdims=True)
            first = part * ROWS + i * CHUNK
            grad_rows[first : first + CHUNK, :] = jnp.broadcast_to(column, (CHUNK, 128))

    def backward(t, head_sum):
        rows = pl.ds(pl.multiple_of(t * SUB, SUB), SUB)
        g = jnp.concatenate([grad_rows[rows, :]] * (HALF // 128), 1)
        back[rows, :] = (g * slope[rows, :]).astype(BF16)
        return head_sum + jnp.sum((g * head_in[rows, :]).reshape(SUB // 8, 8, HALF), 0)

    head_sum = lax.fori_loop(0, 2 * ROWS // SUB, backward, jnp.zeros((8, HALF), F32), unroll=2)
    vec_x[0, :, :HALF] = jnp.sum(head_sum, 0, keepdims=True)
    vec_x[0, :, HALF:] = jnp.broadcast_to(loss_here, (1, 128))

    def vec_copies(axis, buf, sem, count):
        return [
            remote(buf.at[0], buf.at[d], sem.at[0, d], sem.at[1, d], **{axis: at(axis, d)})
            for d in range(1, count)
        ]

    def vec_sum(buf, me, count):
        result = buf[me]
        for q in range(1, count):
            result = result + buf[lax.rem(me - q + count, count)]
        return result

    vec_x_out = vec_copies(X, vec_x, vec_x_sem, 4)
    vec_y_out = vec_copies(Y, vec_y, vec_y_sem, 4)
    vec_z_out = vec_copies(Z, vec_z, vec_z_sem, 8)
    vec_c_out = remote(vec_c.at[0], vec_c.at[1], vec_c_sem.at[0], vec_c_sem.at[1], **{C: other})
    for copy in vec_x_out:
        copy.start()

    def vec_step_y():
        for copy in vec_x_out:
            copy.wait_recv()
        vec_y[0] = vec_sum(vec_x, x, 4)
        for copy in vec_y_out:
            copy.start()

    def vec_step_z():
        for copy in vec_y_out:
            copy.wait_recv()
        vec_z[0] = vec_sum(vec_y, y, 4)
        for copy in vec_z_out:
            copy.start()

    def vec_step_c():
        for copy in vec_z_out:
            copy.wait_recv()
        vec_c[0] = vec_sum(vec_z, z, 8)
        vec_c_out.start()

    def target_z(k):
        return lax.rem(z + jnp.where(lax.rem(k, 2) == 1, 4 - (k + 1) // 2, 4 + k // 2), 8)

    branches = (
        (0, X, Y, x, y, gx, far_x, near_x, mid_x, last_x),
        (1, Y, X, y, x, gy, far_y, near_y, mid_y, last_y),
    )

    def held(n):
        return pl.ds(0, len(GROUPS[n]))

    def far_copies(n, b):
        i, axis, _, me, _, g, far, _, _, _ = branches[b]
        return [
            remote(
                g.at[n, at(axis, 2), pl.ds(2 * s, 2), held(n)],
                far.at[n, s, :, held(n)],
                far_sem.at[0, i, n, s],
                far_sem.at[1, i, n, s],
                **{axis: at(axis, 1 - 2 * s)},
            )
            for s in range(2)
        ]

    def near_copies(n, b):
        i, axis, _, me, _, g, _, near, _, _ = branches[b]
        return [
            remote(
                g.at[n, at(axis, 1 - 2 * s), :, held(n)],
                near.at[n, s, :, held(n)],
                near_sem.at[0, i, n, s],
                near_sem.at[1, i, n, s],
                **{axis: at(axis, 1 - 2 * s)},
            )
            for s in range(2)
        ]

    def mid_copies(n, b):
        i, _, axis, me, _, g, _, _, mid, _ = branches[b]
        return [
            remote(
                g.at[n, me, at(axis, d), held(n)],
                mid.at[n, d - 1, held(n)],
                mid_sem.at[0, i, n, d - 1],
                mid_sem.at[1, i, n, d - 1],
                **{axis: at(axis, d)},
            )
            for d in range(1, 4)
        ]

    def last_copy(k, b):
        i, _, _, me, me2, g, _, _, _, last = branches[b]
        return remote(
            g.at[(k + 1) // 2, me, me2, 0 if k == 0 else (k + 1) % 2],
            last.at[k],
            last_sem.at[0, i, k],
            last_sem.at[1, i, k],
            **{Z: target_z(k)},
        )

    def block(n, d):
        k = GROUPS[n][0] + d
        columns = pl.ds(pl.multiple_of(target_z(k) * 256, 256), 256)
        result = lax.dot_general(
            normed[:, columns],
            back[...],
            (((0,), (0,)), ((), ())),
            preferred_element_type=F32,
        ).astype(BF16)
        for i in range(4):
            for j in range(4):
                part = result[i * 64 + j * 16 : i * 64 + j * 16 + 16, :]
                gx[n, i, j, d] = part[:, :AHEAD]
                gy[n, j, i, d] = part[:, AHEAD : 2 * AHEAD]
                gz[k, i, j] = part[:, 2 * AHEAD :]

    def stage_block(n):
        def one(d, carry):
            block(n, d)
            return carry

        lax.fori_loop(0, len(GROUPS[n]), one, 0)
        for b in range(2):
            for copy in far_copies(n, b):
                copy.start()

    def stage_near(n):
        for b in range(2):
            _, axis, _, _, _, g, far, _, _, _ = branches[b]
            copies = near_copies(n, b)
            for s, arrived in enumerate(far_copies(n, b)):
                arrived.wait_recv()
                ref = g.at[n, at(axis, 1 - 2 * s), pl.ds(2 * s, 2), held(n)]
                ref[...] = (
                    ref[...].astype(F32) + far[n, s, :, held(n)].astype(F32)
                ).astype(BF16)
                copies[s].start()

    def stage_mid(n):
        for b in range(2):
            _, _, _, me, _, g, _, near, _, _ = branches[b]
            for copy in near_copies(n, b):
                copy.wait_recv()
            ref = g.at[n, me, :, held(n)]
            ref[...] = (
                ref[...].astype(F32)
                + near[n, 0, :, held(n)].astype(F32)
                + near[n, 1, :, held(n)].astype(F32)
            ).astype(BF16)
            for copy in mid_copies(n, b):
                copy.start()

    def mid_total(n, b):
        _, _, _, me, me2, g, _, _, mid, _ = branches[b]
        for copy in mid_copies(n, b):
            copy.wait_recv()
        result = g[n, me, me2, held(n)].astype(F32)
        for d in range(3):
            result = result + mid[n, d, held(n)].astype(F32)
        return result

    def stage_last(n):
        for b in range(2):
            _, _, _, me, me2, g, _, _, _, _ = branches[b]
            g[n, me, me2, held(n)] = mid_total(n, b).astype(BF16)
            for k in GROUPS[n]:
                last_copy(k, b).start()

    far_z_out = [
        remote(
            gz.at[PLUS[4], pl.ds(2 * s, 2)],
            far_z.at[s],
            far_z_sem.at[0, s],
            far_z_sem.at[1, s],
            **{Z: at(Z, 1 - 2 * s)},
        )
        for s in range(2)
    ]

    def near_z_copy(j, s, h):
        return remote(
            gz.at[(PLUS, MINUS)[s][j], pl.ds(2 * h, 2)],
            near_z.at[s, j - 1, pl.ds(2 * h, 2)],
            near_z_sem.at[0, s, j - 1, h],
            near_z_sem.at[1, s, j - 1, h],
            **{Z: at(Z, 1 - 2 * s)},
        )

    def stage_z(j, late):
        for s in range(2):
            h = s if late else 1 - s
            ref = gz.at[(PLUS, MINUS)[s][j], pl.ds(2 * h, 2)]
            arrived = None
            if j < 3:
                near_z_copy(j + 1, s, h).wait_recv()
                arrived = near_z[s, j, pl.ds(2 * h, 2)]
            elif late:
                far_z_out[s].wait_recv()
                arrived = far_z[s]
            if arrived is not None:
                ref[...] = (ref[...].astype(F32) + arrived.astype(F32)).astype(BF16)
            near_z_copy(j, s, h).start()

    plane_z_out = [
        remote(
            gz.at[7, at(X, dx), at(Y, dy)],
            plane_z.at[dx * 4 + dy],
            plane_z_sem.at[0, dx * 4 + dy],
            plane_z_sem.at[1, dx * 4 + dy],
            **{X: at(X, dx), Y: at(Y, dy)},
        )
        for dx, dy in plane
    ]

    def stage_z_plane():
        for s in range(2):
            for h in range(2):
                near_z_copy(1, s, h).wait_recv()
        gz[7] = (
            gz[7].astype(F32) + near_z[0, 0].astype(F32) + near_z[1, 0].astype(F32)
        ).astype(BF16)
        for copy in plane_z_out:
            copy.start()

    stage_block(0)
    for copy in far_z_out:
        copy.start()
    stage_block(1)
    stage_z(3, 0)
    stage_block(2)
    vec_step_y()
    stage_near(0)
    stage_z(3, 1)
    stage_block(3)
    stage_block(4)
    stage_near(1)
    stage_z(2, 0)
    stage_near(2)
    stage_z(2, 1)
    stage_mid(0)
    vec_step_z()
    stage_near(3)
    stage_near(4)
    stage_z(1, 0)
    stage_mid(1)
    stage_z(1, 1)
    stage_mid(2)
    stage_last(0)
    vec_step_c()
    stage_mid(3)
    stage_last(1)
    stage_z_plane()
    stage_mid(4)
    stage_last(2)
    stage_last(3)

    for b in range(2):
        total[:, b * AHEAD : (b + 1) * AHEAD] = mid_total(4, b)[0]
    for b in range(2):
        last = branches[b][9]
        result = total[:, b * AHEAD : (b + 1) * AHEAD]
        for k in range(7):
            last_copy(k, b).wait_recv()
            result = result + last[k].astype(F32)
        total[:, b * AHEAD : (b + 1) * AHEAD] = result
    result = gz[7, x, y].astype(F32)
    for n, copy in enumerate(plane_z_out):
        copy.wait_recv()
        result = result + plane_z[n + 1].astype(F32)
    total[:, 2 * AHEAD :] = result
    total_out = remote(
        total.at[pl.ds(pl.multiple_of(other * 8, 8), 8)],
        total_peer,
        total_sem.at[0],
        total_sem.at[1],
        **{C: other},
    )
    total_out.start()

    vec_c_out.wait_recv()
    grad_head_ref[:, half] = vec_c[0, :, :HALF]
    grad_head_ref[:, other_half] = vec_c[1, :, :HALF]
    loss_ref[...] = (vec_c[0, :, HALF:] + vec_c[1, :, HALF:]) * (1.0 / (STATES * 8))
    grad_ref[:, half] = total[pl.ds(pl.multiple_of(c * 8, 8), 8), :]

    sent = [pair, scores_out, vec_c_out]
    sent += state_out + lse_out + vec_x_out + vec_y_out + vec_z_out
    sent += far_z_out + plane_z_out
    sent += [rows_out(i) for i in range(3)]
    sent += [near_z_copy(j, s, h) for j in range(1, 4) for s in range(2) for h in range(2)]
    for copy in sent:
        copy.wait_send()

    for b in range(2):
        for n in range(len(GROUPS)):
            for copy in far_copies(n, b) + near_copies(n, b) + mid_copies(n, b):
                copy.wait_send()
        for k in range(7):
            last_copy(k, b).wait_send()
    total_out.wait()
    grad_ref[:, other_half] = total_peer[...]


def deliver(grad_in, grad_head_in, lse_in, loss_in, grad_out, grad_head_out, lse_out, loss_out):
    grad_out[...] = grad_in[...]
    grad_head_out[...] = grad_head_in[...]
    lse_out[...] = lse_in[...]
    loss_out[...] = loss_in[:, :1]


def body(state_features, action_features, targets, w_hidden, w_head):
    vmem = pl.BlockSpec(memory_space=pltpu.VMEM)
    anywhere = pl.BlockSpec(memory_space=pl.ANY)
    dma = pltpu.SemaphoreType.DMA
    scratch = [
        pltpu.VMEM((WIDTH, HALF), BF16),
        pltpu.VMEM((ROWS, WIDTH), BF16),
        pltpu.VMEM((64, 128), BF16),
        pltpu.VMEM((2, 16, 64, 128), BF16),
        pltpu.VMEM((STATES, WIDTH), F32),
        pltpu.VMEM((2 * ROWS, WIDTH), BF16),
        pltpu.VMEM((CHUNK, HALF), F32),
        pltpu.VMEM((CHUNK, HALF), F32),
        pltpu.VMEM((2 * ROWS, HALF), F32),
        pltpu.VMEM((2 * ROWS, HALF), F32),
        pltpu.VMEM((2 * ROWS, HALF), BF16),
        pltpu.VMEM((2 * ROWS, 128), F32),
        pltpu.VMEM((STATES, 128), F32),
        pltpu.VMEM((STATES, 128), F32),
        pltpu.VMEM((STATES, 128), F32),
        pltpu.VMEM((2 * ROWS, 128), F32),
        pltpu.VMEM((16, 1, 128), F32),
        pltpu.VMEM((4, 1, VECTOR), F32),
        pltpu.VMEM((4, 1, VECTOR), F32),
        pltpu.VMEM((8, 1, VECTOR), F32),
        pltpu.VMEM((2, 1, VECTOR), F32),
        pltpu.VMEM((len(GROUPS), 4, 4, DEPTH, 16, AHEAD), BF16),
        pltpu.VMEM((len(GROUPS), 4, 4, DEPTH, 16, AHEAD), BF16),
        pltpu.VMEM((8, 4, 4, 16, LAST), BF16),
        pltpu.VMEM((len(GROUPS), 2, 2, DEPTH, 16, AHEAD), BF16),
        pltpu.VMEM((len(GROUPS), 2, 2, DEPTH, 16, AHEAD), BF16),
        pltpu.VMEM((len(GROUPS), 2, 4, DEPTH, 16, AHEAD), BF16),
        pltpu.VMEM((len(GROUPS), 2, 4, DEPTH, 16, AHEAD), BF16),
        pltpu.VMEM((len(GROUPS), 3, DEPTH, 16, AHEAD), BF16),
        pltpu.VMEM((len(GROUPS), 3, DEPTH, 16, AHEAD), BF16),
        pltpu.VMEM((8, 16, AHEAD), BF16),
        pltpu.VMEM((8, 16, AHEAD), BF16),
        pltpu.VMEM((2, 2, 4, 16, LAST), BF16),
        pltpu.VMEM((2, 3, 4, 4, 16, LAST), BF16),
        pltpu.VMEM((16, 16, LAST), BF16),
        pltpu.VMEM((16, HALF), F32),
        pltpu.VMEM((8, HALF), F32),
        dma((4,)),
        dma((2,)),
        dma((2, 16)),
        dma((2, 3)),
        dma((2,)),
        dma((2, 16)),
        dma((2, 4)),
        dma((2, 4)),
        dma((2, 8)),
        dma((2,)),
        dma((2, 2, len(GROUPS), 2)),
        dma((2, 2, len(GROUPS), 2)),
        dma((2, 2, len(GROUPS), 3)),
        dma((2, 2, 8)),
        dma((2, 2)),
        dma((2, 2, 3, 2)),
        dma((2, 16)),
        dma((2,)),
    ]
    grad, grad_head, lse, loss = pl.pallas_call(
        kernel,
        out_shape=(
            jax.ShapeDtypeStruct((8, WIDTH), F32),
            jax.ShapeDtypeStruct((1, WIDTH), F32),
            jax.ShapeDtypeStruct((1, STATES), F32),
            jax.ShapeDtypeStruct((1, 128), F32),
        ),
        in_specs=[vmem, anywhere, vmem, anywhere, vmem],
        out_specs=(vmem,) * 4,
        scratch_shapes=scratch,
        compiler_params=pltpu.CompilerParams(
            collective_id=0, has_side_effects=True, vmem_limit_bytes=62 * 1024 * 1024
        ),
        name="critic",
    )(
        state_features.T,
        action_features.reshape(ROWS, WIDTH),
        targets.reshape(1, STATES),
        w_hidden,
        w_head.reshape(1, WIDTH),
    )
    grad, grad_head, lse, loss = pl.pallas_call(
        deliver,
        out_shape=(
            jax.ShapeDtypeStruct((8, WIDTH), F32),
            jax.ShapeDtypeStruct((1, WIDTH), F32),
            jax.ShapeDtypeStruct((1, STATES), F32),
            jax.ShapeDtypeStruct((1, 1), F32),
        ),
        in_specs=[vmem] * 4,
        out_specs=(vmem,) * 4,
        name="deliver",
    )(grad, grad_head, lse, loss)
    return grad, grad_head.reshape(WIDTH), lse.reshape(STATES), loss.reshape(())


def solution(mesh):
    finer = Mesh(mesh.devices.reshape(8, 4, 4, 2), (Z, X, Y, C))
    return jax.shard_map(
        body,
        mesh=finer,
        in_specs=(P(Z, ACT), P(Z, ACT, None), P(Z), P(), P()),
        out_specs=(P(STATE_ACT, None), P(), P(Z), P()),
        check_vma=False,
    )
```

time: 95.8 us -> 73.3 us (0.77)
  Pallas kernels: 87.8 us -> 72.5 us
  local copies, waits for them, and re-layouts: 5.29 us -> 0 us
  between operations: 2.46 us -> 0.64 us
    pallas_call x1, Pallas kernels: 87.8 us -> 70.9 us  [body(): pl.pallas_call(kernel, out_shape=(jax.ShapeDtypeStruct((8, WIDTH), F32),...]
    unnamed x4 -> x0, local copies, waits for them, and re-layouts: 5.29 us -> none
    pallas_call x0 -> x1, Pallas kernels: none -> 1.5 us  [body(): pl.pallas_call(deliver, out_shape=(jax.ShapeDtypeStruct((8, WIDTH), F32),...]
where the time goes in v2:
time: 73.3 us; the launch traced here: 73.1 us
  Pallas kernels  72.5 us (99%)
    pallas_call x1, Pallas kernels, body(): pl.pallas_call(kernel, out_shape=(jax.ShapeDtypeStruct((8, WIDTH), F32),...  70.9 us
    pallas_call x1, Pallas kernels, body(): pl.pallas_call(deliver, out_shape=(jax.ShapeDtypeStruct((8, WIDTH), F32),...  1.5 us

profile of v2, /device:TPU:1, one launch (start us, length us, event | category | flops | bytes accessed | tf_op | source)
XLA Modules:
  0.0 73.1 jit_solution(5158760598908628381)
XLA Ops:
  0.6 70.9 %critic.1 = (f32[8,2048]{1,0:T(8,128)}, f32[1,2048]{1,0:T(1,128)}, f32[1,96]{1,0:T(1,128)}, f32[1,128]{1,0:T(1,128)}) custom-call(bf16[64,96]{1,0:T(8,128)(2,1)} %bitcast.8, bf16[768,2048]{1,0:T(8,128)(2,1)} %bitcast.7, f32[1,96]{1,0:T(1,128)} %bitcast.10, bf16[2048,2048]{1,0:T(8,128)(2,1)} %w_hbm.1, f32[1,2048]{1,0:T(1,128)} %bitcast.9), custom_call_target="tpu_custom_call" | custom-call | tf_op jit(solution)/shard_map/critic/pallas_call | solution.py:690
  71.6 1.5 %deliver.1 = (f32[8,2048]{1,0:T(8,128)}, f32[1,2048]{1,0:T(1,128)}, f32[1,96]{1,0:T(1,128)}, f32[1,1]{1,0:T(1,128)}) custom-call(f32[8,2048]{1,0:T(8,128)} %get-tuple-element.12.grad_in, f32[1,2048]{1,0:T(1,128)} %get-tuple-element.13.grad_head_in, f32[1,96]{1,0:T(1,128)} %get-tuple-element.14.lse_in, f32[1,128]{1,0:T(1,128)} %get-tuple-element.15.loss_in), custom_call_target="tpu_custom_call" | custom-call | tf_op jit(solution)/shard_map/deliver/pallas_call | solution.py:712

commit v3 on v2

--- a/solution.py
+++ b/solution.py
@@ -42,6 +42,10 @@
     )
 
 
+def take(ref, sem):
+    pltpu.make_async_copy(ref, ref, sem).wait()
+
+
 def kernel(
     state_ref,
     act_hbm,
@@ -58,8 +62,8 @@
     state_all,
     state_f32,
     normed,
-    preact_a,
-    preact_b,
+    state_pre,
+    scale,
     head_in,
     slope,
     back,
@@ -92,7 +96,9 @@
     sem_in,
     pair_sem,
     state_sem,
+    acts_sem,
     rows_sem,
+    scale_sem,
     score_sem,
     lse_sem,
     vec_x_sem,
@@ -149,16 +155,36 @@
         remote(
             state_own,
             state_all.at[c, dx * 4 + dy],
-            state_sem.at[0, dx * 4 + dy],
-            state_sem.at[1, dx * 4 + dy],
+            state_sem.at[0],
+            state_sem.at[1],
             **{X: at(X, dx), Y: at(Y, dy)},
         )
         for dx, dy in plane
     ]
     for copy in state_out:
         copy.start()
-    for copy in state_out:
-        copy.wait_recv()
+
+    def shared(ref, sem, i):
+        return remote(
+            ref.at[pl.ds(i * CHUNK, CHUNK)],
+            ref.at[pl.ds(ROWS + i * CHUNK, CHUNK)],
+            sem.at[0],
+            sem.at[1 + i],
+            **{C: other},
+        )
+
+    acts_out = [shared(act_buf, acts_sem, i) for i in range(3)]
+    for i in range(3):
+        act_in[i].wait()
+        acts_out[i].start()
+    w_in.wait()
+    for i in range(6):
+        if i >= 3:
+            acts_out[i - 3].wait_recv()
+        rows = slice(i * CHUNK, (i + 1) * CHUNK)
+        head_in[rows, :] = jnp.dot(act_buf[rows, :], w_buf[...], preferred_element_type=F32)
+
+    take(state_all.at[0, pl.ds(0, 15)], state_sem.at[1])
     pair = remote(state_all.at[c], state_all.at[c], pair_sem.at[0], pair_sem.at[1], **{C: other})
     pair_in = remote(
         state_all.at[other], state_all.at[other], pair_sem.at[0], pair_sem.at[1], **{C: other}
@@ -170,14 +196,12 @@
         tile = jnp.concatenate([state_all[0, slot], state_all[1, slot]], 0).astype(F32)
         state_f32[:, j * 128 : (j + 1) * 128] = tile.T[:STATES, :]
 
-    def rows_out(i):
-        return remote(
-            normed.at[pl.ds(i * CHUNK, CHUNK)],
-            normed.at[pl.ds(ROWS + i * CHUNK, CHUNK)],
-            rows_sem.at[0, i],
-            rows_sem.at[1, i],
-            **{C: other},
-        )
+    state_pre[...] = jnp.dot(
+        state_f32[...].astype(BF16), w_buf[...], preferred_element_type=F32
+    )
+
+    rows_out = [shared(normed, rows_sem, i) for i in range(3)]
+    scale_out = [shared(scale, scale_sem, i) for i in range(3)]
 
     def mixture(u, j):
         tile = slice(j * 128, (j + 1) * 128)
@@ -186,7 +210,6 @@
         return lines + act_buf[u * 64 : u * 64 + 64, tile].astype(F32)
 
     def normalise(i):
-        act_in[i].wait()
         for u in range(i * 4, i * 4 + 4):
             rows = slice(u * 64, u * 64 + 64)
             sums = None
@@ -195,22 +218,22 @@
                 sums = m * m if sums is None else sums + m * m
             mean = jnp.sum(sums, -1, keepdims=True) * (1.0 / WIDTH)
             factor = jnp.broadcast_to(lax.rsqrt(mean + norm_epsilon), (64, 128))
+            scale[rows, :] = factor
             for j in range(WIDTH // 128):
                 normed[rows, j * 128 : (j + 1) * 128] = (mixture(u, j) * factor).astype(BF16)
 
     lane8 = lax.broadcasted_iota(jnp.int32, (8, 128), 1)
     row8 = lax.broadcasted_iota(jnp.int32, (8, 128), 0)
 
-    def product(i, buf):
-        buf[...] = jnp.dot(
-            normed[i * CHUNK : (i + 1) * CHUNK, :], w_buf[...], preferred_element_type=F32
-        )
-
-    def finish(i, buf):
+    def finish(i):
         w = head_ref[:, half]
         for t in range(CHUNK // SUB):
             rows = slice(i * CHUNK + t * SUB, i * CHUNK + (t + 1) * SUB)
-            p = buf[t * SUB : (t + 1) * SUB, :]
+            state = (i % 3) * (CHUNK // 8) + t * (SUB // 8)
+            line = state_pre[state : state + SUB // 8, :]
+            line = jnp.broadcast_to(line[:, None, :], (SUB // 8, 8, HALF)).reshape(SUB, HALF)
+            factor = jnp.concatenate([scale[rows, :]] * (HALF // 128), 1)
+            p = factor * (head_in[rows, :] + line)
             g = 0.5 * jnp.tanh(0.5 * p) + 0.5
             pg = p * g
             h = normed[rows, half].astype(F32) + pg
@@ -222,20 +245,15 @@
                 sums = sums + hw[:, j * 128 : (j + 1) * 128]
             score_lanes[rows, :] = sums
 
-    buffers = (preact_a, preact_b)
-    normalise(0)
-    rows_out(0).start()
-    w_in.wait()
+    for i in range(3):
+        normalise(i)
+        rows_out[i].start()
+        scale_out[i].start()
     for i in range(6):
         if i >= 3:
-            rows_out(i - 3).wait_recv()
-        product(i, buffers[i % 2])
-        if i < 2:
-            normalise(i + 1)
-            rows_out(i + 1).start()
-        if i > 0:
-            finish(i - 1, buffers[(i - 1) % 2])
-    finish(5, buffers[1])
+            rows_out[i - 3].wait_recv()
+            scale_out[i - 3].wait_recv()
+        finish(i)
 
     for i in range(3):
         states = 0.0
@@ -262,16 +280,15 @@
         remote(
             lse_all.at[0],
             lse_all.at[dx * 4 + dy],
-            lse_sem.at[0, dx * 4 + dy],
-            lse_sem.at[1, dx * 4 + dy],
+            lse_sem.at[0],
+            lse_sem.at[1],
             **{X: at(X, dx), Y: at(Y, dy)},
         )
         for dx, dy in plane
     ]
     for copy in lse_out:
         copy.start()
-    for copy in lse_out:
-        copy.wait_recv()
+    take(lse_all.at[pl.ds(0, 15)], lse_sem.at[1])
     parts = [
         lse_all[lax.rem(x - j // 4 + 4, 4) * 4 + lax.rem(y - j % 4 + 4, 4)] for j in range(16)
     ]
@@ -319,7 +336,7 @@
 
     def vec_copies(axis, buf, sem, count):
         return [
-            remote(buf.at[0], buf.at[d], sem.at[0, d], sem.at[1, d], **{axis: at(axis, d)})
+            remote(buf.at[0], buf.at[d], sem.at[0], sem.at[1], **{axis: at(axis, d)})
             for d in range(1, count)
         ]
 
@@ -337,22 +354,19 @@
         copy.start()
 
     def vec_step_y():
-        for copy in vec_x_out:
-            copy.wait_recv()
+        take(vec_x.at[pl.ds(0, 3)], vec_x_sem.at[1])
         vec_y[0] = vec_sum(vec_x, x, 4)
         for copy in vec_y_out:
             copy.start()
 
     def vec_step_z():
-        for copy in vec_y_out:
-            copy.wait_recv()
+        take(vec_y.at[pl.ds(0, 3)], vec_y_sem.at[1])
         vec_z[0] = vec_sum(vec_y, y, 4)
         for copy in vec_z_out:
             copy.start()
 
     def vec_step_c():
-        for copy in vec_z_out:
-            copy.wait_recv()
+        take(vec_z.at[pl.ds(0, 7)], vec_z_sem.at[1])
         vec_c[0] = vec_sum(vec_z, z, 8)
         vec_c_out.start()
 
@@ -373,8 +387,8 @@
             remote(
                 g.at[n, at(axis, 2), pl.ds(2 * s, 2), held(n)],
                 far.at[n, s, :, held(n)],
-                far_sem.at[0, i, n, s],
-                far_sem.at[1, i, n, s],
+                far_sem.at[i, 0],
+                far_sem.at[i, 1 + 2 * n + s],
                 **{axis: at(axis, 1 - 2 * s)},
             )
             for s in range(2)
@@ -386,8 +400,8 @@
             remote(
                 g.at[n, at(axis, 1 - 2 * s), :, held(n)],
                 near.at[n, s, :, held(n)],
-                near_sem.at[0, i, n, s],
-                near_sem.at[1, i, n, s],
+                near_sem.at[i, 0],
+                near_sem.at[i, 1 + n],
                 **{axis: at(axis, 1 - 2 * s)},
             )
             for s in range(2)
@@ -399,8 +413,8 @@
             remote(
                 g.at[n, me, at(axis, d), held(n)],
                 mid.at[n, d - 1, held(n)],
-                mid_sem.at[0, i, n, d - 1],
-                mid_sem.at[1, i, n, d - 1],
+                mid_sem.at[i, 0],
+                mid_sem.at[i, 1 + n],
                 **{axis: at(axis, d)},
             )
             for d in range(1, 4)
@@ -411,8 +425,8 @@
         return remote(
             g.at[(k + 1) // 2, me, me2, 0 if k == 0 else (k + 1) % 2],
             last.at[k],
-            last_sem.at[0, i, k],
-            last_sem.at[1, i, k],
+            last_sem.at[i, 0],
+            last_sem.at[i, 1],
             **{Z: target_z(k)},
         )
 
@@ -457,8 +471,7 @@
     def stage_mid(n):
         for b in range(2):
             _, _, _, me, _, g, _, near, _, _ = branches[b]
-            for copy in near_copies(n, b):
-                copy.wait_recv()
+            take(near.at[n, :, :, held(n)], near_sem.at[b, 1 + n])
             ref = g.at[n, me, :, held(n)]
             ref[...] = (
                 ref[...].astype(F32)
@@ -470,8 +483,7 @@
 
     def mid_total(n, b):
         _, _, _, me, me2, g, _, _, mid, _ = branches[b]
-        for copy in mid_copies(n, b):
-            copy.wait_recv()
+        take(mid.at[n, :, held(n)], mid_sem.at[b, 1 + n])
         result = g[n, me, me2, held(n)].astype(F32)
         for d in range(3):
             result = result + mid[n, d, held(n)].astype(F32)
@@ -488,8 +500,8 @@
         remote(
             gz.at[PLUS[4], pl.ds(2 * s, 2)],
             far_z.at[s],
-            far_z_sem.at[0, s],
-            far_z_sem.at[1, s],
+            far_z_sem.at[0],
+            far_z_sem.at[1 + s],
             **{Z: at(Z, 1 - 2 * s)},
         )
         for s in range(2)
@@ -499,8 +511,8 @@
         return remote(
             gz.at[(PLUS, MINUS)[s][j], pl.ds(2 * h, 2)],
             near_z.at[s, j - 1, pl.ds(2 * h, 2)],
-            near_z_sem.at[0, s, j - 1, h],
-            near_z_sem.at[1, s, j - 1, h],
+            near_z_sem.at[0],
+            near_z_sem.at[1 + s * 6 + (j - 1) * 2 + h],
             **{Z: at(Z, 1 - 2 * s)},
         )
 
@@ -523,8 +535,8 @@
         remote(
             gz.at[7, at(X, dx), at(Y, dy)],
             plane_z.at[dx * 4 + dy],
-            plane_z_sem.at[0, dx * 4 + dy],
-            plane_z_sem.at[1, dx * 4 + dy],
+            plane_z_sem.at[0],
+            plane_z_sem.at[1],
             **{X: at(X, dx), Y: at(Y, dy)},
         )
         for dx, dy in plane
@@ -566,9 +578,9 @@
     stage_last(0)
     vec_step_c()
     stage_mid(3)
-    stage_last(1)
     stage_z_plane()
     stage_mid(4)
+    stage_last(1)
     stage_last(2)
     stage_last(3)
 
@@ -577,14 +589,14 @@
     for b in range(2):
         last = branches[b][9]
         result = total[:, b * AHEAD : (b + 1) * AHEAD]
+        take(last.at[pl.ds(0, 7)], last_sem.at[b, 1])
         for k in range(7):
-            last_copy(k, b).wait_recv()
             result = result + last[k].astype(F32)
         total[:, b * AHEAD : (b + 1) * AHEAD] = result
     result = gz[7, x, y].astype(F32)
-    for n, copy in enumerate(plane_z_out):
-        copy.wait_recv()
-        result = result + plane_z[n + 1].astype(F32)
+    take(plane_z.at[pl.ds(0, 15)], plane_z_sem.at[1])
+    for n in range(1, 16):
+        result = result + plane_z[n].astype(F32)
     total[:, 2 * AHEAD :] = result
     total_out = remote(
         total.at[pl.ds(pl.multiple_of(other * 8, 8), 8)],
@@ -601,20 +613,27 @@
     loss_ref[...] = (vec_c[0, :, HALF:] + vec_c[1, :, HALF:]) * (1.0 / (STATES * 8))
     grad_ref[:, half] = total[pl.ds(pl.multiple_of(c * 8, 8), 8), :]
 
-    sent = [pair, scores_out, vec_c_out]
-    sent += state_out + lse_out + vec_x_out + vec_y_out + vec_z_out
-    sent += far_z_out + plane_z_out
-    sent += [rows_out(i) for i in range(3)]
-    sent += [near_z_copy(j, s, h) for j in range(1, 4) for s in range(2) for h in range(2)]
-    for copy in sent:
+    for copy in (pair, scores_out, vec_c_out):
         copy.wait_send()
-
+    for ref, sem in (
+        (state_all.at[0, pl.ds(0, 15)], state_sem),
+        (lse_all.at[pl.ds(0, 15)], lse_sem),
+        (act_buf.at[pl.ds(0, ROWS)], acts_sem),
+        (normed.at[pl.ds(0, ROWS)], rows_sem),
+        (scale.at[pl.ds(0, ROWS)], scale_sem),
+        (vec_x.at[pl.ds(0, 3)], vec_x_sem),
+        (vec_y.at[pl.ds(0, 3)], vec_y_sem),
+        (vec_z.at[pl.ds(0, 7)], vec_z_sem),
+        (gz.at[0], far_z_sem),
+        (gz.at[pl.ds(0, 6)], near_z_sem),
+        (plane_z.at[pl.ds(0, 15)], plane_z_sem),
+    ):
+        take(ref, sem.at[0])
     for b in range(2):
-        for n in range(len(GROUPS)):
-            for copy in far_copies(n, b) + near_copies(n, b) + mid_copies(n, b):
-                copy.wait_send()
-        for k in range(7):
-            last_copy(k, b).wait_send()
+        take(gx.at[0], far_sem.at[b, 0])
+        take(gx.at[pl.ds(0, 2)], near_sem.at[b, 0])
+        take(gx.at[0, pl.ds(0, 3)], mid_sem.at[b, 0])
+        take(last_x.at[pl.ds(0, 7)], last_sem.at[b, 0])
     total_out.wait()
     grad_ref[:, other_half] = total_peer[...]
 
@@ -632,13 +651,13 @@
     dma = pltpu.SemaphoreType.DMA
     scratch = [
         pltpu.VMEM((WIDTH, HALF), BF16),
-        pltpu.VMEM((ROWS, WIDTH), BF16),
+        pltpu.VMEM((2 * ROWS, WIDTH), BF16),
         pltpu.VMEM((64, 128), BF16),
         pltpu.VMEM((2, 16, 64, 128), BF16),
         pltpu.VMEM((STATES, WIDTH), F32),
         pltpu.VMEM((2 * ROWS, WIDTH), BF16),
-        pltpu.VMEM((CHUNK, HALF), F32),
-        pltpu.VMEM((CHUNK, HALF), F32),
+        pltpu.VMEM((STATES, HALF), F32),
+        pltpu.VMEM((2 * ROWS, 128), F32),
         pltpu.VMEM((2 * ROWS, HALF), F32),
         pltpu.VMEM((2 * ROWS, HALF), F32),
         pltpu.VMEM((2 * ROWS, HALF), BF16),
@@ -670,21 +689,23 @@
         pltpu.VMEM((8, HALF), F32),
         dma((4,)),
         dma((2,)),
-        dma((2, 16)),
-        dma((2, 3)),
-        dma((2,)),
-        dma((2, 16)),
-        dma((2, 4)),
-        dma((2, 4)),
-        dma((2, 8)),
-        dma((2,)),
-        dma((2, 2, len(GROUPS), 2)),
-        dma((2, 2, len(GROUPS), 2)),
-        dma((2, 2, len(GROUPS), 3)),
-        dma((2, 2, 8)),
+        dma((2,)),
+        dma((4,)),
+        dma((4,)),
+        dma((4,)),
+        dma((2,)),
+        dma((2,)),
+        dma((2,)),
+        dma((2,)),
+        dma((2,)),
+        dma((2,)),
+        dma((2, 1 + 2 * len(GROUPS))),
+        dma((2, 1 + len(GROUPS))),
+        dma((2, 1 + len(GROUPS))),
         dma((2, 2)),
-        dma((2, 2, 3, 2)),
-        dma((2, 16)),
+        dma((3,)),
+        dma((13,)),
+        dma((2,)),
         dma((2,)),
     ]
     grad, grad_head, lse, loss = pl.pallas_call(

time: 73.3 us -> 67.1 us (0.915)
  Pallas kernels: 72.5 us -> 66.3 us
    pallas_call x1, Pallas kernels: 70.9 us -> 64.8 us  [body(): pl.pallas_call(kernel, out_shape=(jax.ShapeDtypeStruct((8, WIDTH), F32),...]
where the time goes in v3:
time: 67.1 us; the launch traced here: 66.9 us
  Pallas kernels  66.3 us (99%)
    pallas_call x1, Pallas kernels, body(): pl.pallas_call(kernel, out_shape=(jax.ShapeDtypeStruct((8, WIDTH), F32),...  64.8 us
    pallas_call x1, Pallas kernels, body(): pl.pallas_call(deliver, out_shape=(jax.ShapeDtypeStruct((8, WIDTH), F32),...  1.5 us

profile of v3, /device:TPU:1, one launch (start us, length us, event | category | flops | bytes accessed | tf_op | source)
XLA Modules:
  0.0 66.9 jit_solution(1679894871875058131)
XLA Ops:
  0.6 64.8 %critic.1 = (f32[8,2048]{1,0:T(8,128)}, f32[1,2048]{1,0:T(1,128)}, f32[1,96]{1,0:T(1,128)}, f32[1,128]{1,0:T(1,128)}) custom-call(bf16[64,96]{1,0:T(8,128)(2,1)} %bitcast.8, bf16[768,2048]{1,0:T(8,128)(2,1)} %bitcast.7, f32[1,96]{1,0:T(1,128)} %bitcast.10, bf16[2048,2048]{1,0:T(8,128)(2,1)} %w_hbm.1, f32[1,2048]{1,0:T(1,128)} %bitcast.9), custom_call_target="tpu_custom_call" | custom-call | tf_op jit(solution)/shard_map/critic/pallas_call | solution.py:711
  65.4 1.5 %deliver.1 = (f32[8,2048]{1,0:T(8,128)}, f32[1,2048]{1,0:T(1,128)}, f32[1,96]{1,0:T(1,128)}, f32[1,1]{1,0:T(1,128)}) custom-call(f32[8,2048]{1,0:T(8,128)} %get-tuple-element.12.grad_in, f32[1,2048]{1,0:T(1,128)} %get-tuple-element.13.grad_head_in, f32[1,96]{1,0:T(1,128)} %get-tuple-element.14.lse_in, f32[1,128]{1,0:T(1,128)} %get-tuple-element.15.loss_in), custom_call_target="tpu_custom_call" | custom-call | tf_op jit(solution)/shard_map/deliver/pallas_call | solution.py:733

commit v4 on v3

--- a/solution.py
+++ b/solution.py
@@ -720,7 +720,7 @@
         out_specs=(vmem,) * 4,
         scratch_shapes=scratch,
         compiler_params=pltpu.CompilerParams(
-            collective_id=0, has_side_effects=True, vmem_limit_bytes=62 * 1024 * 1024
+            collective_id=0, has_side_effects=True, vmem_limit_bytes=52 * 1024 * 1024
         ),
         name="critic",
     )(
@@ -740,6 +740,7 @@
         ),
         in_specs=[vmem] * 4,
         out_specs=(vmem,) * 4,
+        compiler_params=pltpu.CompilerParams(vmem_limit_bytes=2 * 1024 * 1024),
         name="deliver",
     )(grad, grad_head, lse, loss)
     return grad, grad_head.reshape(WIDTH), lse.reshape(STATES), loss.reshape(())

time: 67.1 us -> 67.2 us (level)
  Pallas kernels: 66.3 us -> 64.2 us
  local copies, waits for them, and re-layouts: 0 us -> 2.06 us
    unnamed x0 -> x6, local copies, waits for them, and re-layouts: none -> 2.06 us
    pallas_call x1, Pallas kernels: 64.8 us -> 63.6 us  [body(): pl.pallas_call(kernel, out_shape=(jax.ShapeDtypeStruct((8, WIDTH), F32),...]
    pallas_call x1, Pallas kernels: 1.5 us -> 0.64 us  [body(): pl.pallas_call(deliver, out_shape=(jax.ShapeDtypeStruct((8, WIDTH), F32),...]
where the time goes in v4:
time: 67.2 us; the launch traced here: 66.9 us
  Pallas kernels  64.2 us (96%)
  local copies, waits for them, and re-layouts  2.06 us (3%)
    pallas_call x1, Pallas kernels, body(): pl.pallas_call(kernel, out_shape=(jax.ShapeDtypeStruct((8, WIDTH), F32),...  63.6 us
    unnamed x6, local copies, waits for them, and re-layouts  2.06 us

profile of v4, /device:TPU:1, one launch (start us, length us, event | category | flops | bytes accessed | tf_op | source)
XLA Modules:
  0.0 66.9 jit_solution(8323081042067500119)
XLA Ops:
  0.6 0.0 copy-start
  0.6 0.7 %copy-done = bf16[96,64]{0,1:T(8,128)(2,1)S(1)} copy-done((bf16[96,64]{0,1:T(8,128)(2,1)S(1)}, bf16[96,64]{0,1:T(8,128)(2,1)}, u32[]{:S(2)}) %copy-start) | copy-done | bytes 12312
  1.4 0.0 copy-start.1
  1.4 0.7 %copy-done.1 = f32[2048]{0:T(1024)S(1)} copy-done((f32[2048]{0:T(1024)S(1)}, f32[2048]{0:T(1024)}, u32[]{:S(2)}) %copy-start.1) | copy-done | bytes 8216
  2.0 0.0 copy-start.2
  2.0 0.7 copy-done.2
  2.7 63.6 %critic.1 = (f32[8,2048]{1,0:T(8,128)S(1)}, f32[1,2048]{1,0:T(1,128)S(1)}, f32[1,96]{1,0:T(1,128)S(1)}, f32[1,128]{1,0:T(1,128)S(1)}) custom-call(bf16[64,96]{1,0:T(8,128)(2,1)S(1)} %bitcast.7, bf16[768,2048]{1,0:T(8,128)(2,1)} %bitcast.10, f32[1,96]{1,0:T(1,128)S(1)} %bitcast.9, bf16[2048,2048]{1,0:T(8,128)(2,1)} %w_hbm.1, f32[1,2048]{1,0:T(1,128)S(1)} %bitcast.8), custom_call_target="tpu_custom_call" | custom-call | tf_op jit(solution)/shard_map/critic/pallas_call | solution.py:711
  66.3 0.6 deliver.1
Async XLA Ops:
  0.6 0.7 %copy-start = (bf16[96,64]{0,1:T(8,128)(2,1)S(1)}, bf16[96,64]{0,1:T(8,128)(2,1)}, u32[]{:S(2)}) copy-start(bf16[96,64]{0,1:T(8,128)(2,1)} %param.5) | copy-start | bytes 36868
  1.4 0.7 %copy-start.1 = (f32[2048]{0:T(1024)S(1)}, f32[2048]{0:T(1024)}, u32[]{:S(2)}) copy-start(f32[2048]{0:T(1024)} %param.9) | copy-start | bytes 24580
  2.0 0.7 copy-start.2
